TPU v7x, 256 devices: a whole 4x4x8 slice. The times are simulated.
256 devices in a mesh: section: 4 (over z_hi), seq: 64 (over y, z_lo, x, core).
Axes of the slice: x: 4, y: 4, z: 8 (z_hi: 4, z_lo: 2; z = z_hi * 2 + z_lo), core: 2. Of those that a mesh axis runs over, the one named last changes fastest.
Arguments:
- saved: bfloat16 [4, 3, 8192, 2304], P('section', None, 'seq'), may hold values from -16 to 16
- cotangent: bfloat16 [3, 8192, 2304], P(None, 'seq'), may hold values from -0.0390625 to 0.0390625
- slot_table: int32 [4, 3], P('section'), may hold values from 0 to 2, each once within a row
- gain: float32 [4, 2304], P('section'), may hold values from 0.25 to 1.75
- value_weight: bfloat16 [4, 2304, 1024], P('section'), may hold values from -0.125 to 0.125
- out_weight: bfloat16 [4, 2304, 1024], P('section'), may hold values from -0.1875 to 0.1875
Outputs:
- value_grad: float32 [4, 2304, 1024], P('section', 'seq')
- out_grad: float32 [4, 2304, 1024], P('section', 'seq')
- gain_grad: float32 [4, 2304], P('section')
Inputs may be any that keep to these rules, and one draw needn't show every extreme that they name: `slot_table`: each row names every stash slot once.
All inputs are finite; a program needn't handle non-finite values.
Results may differ from a plain program's by a relative error of at most 0.007.
Values may be sent and summed in bfloat16 or wider, within the bound.
A program may use at most 128 MiB of HBM per device.

v0:
```python
import jax
import jax.numpy as jnp
from jax import lax
from jax.sharding import PartitionSpec as P

EPSILON = 1e-06


def passed_along(value, axis, steps):
    count = lax.axis_size(axis)
    first, last = (max(0, -steps), min(count, count - steps))
    return lax.ppermute(value, axis, [(source, source + steps) for source in range(first, last)])


def cut_along(x, dim, devices):
    shape = x.shape
    blocks = x.reshape(*shape[:dim], devices, shape[dim] // devices, *shape[dim + 1 :])
    return jnp.moveaxis(blocks, dim, 0)


def sent_and_summed(x, axis, dim):
    devices = lax.axis_size(axis)
    blocks = lax.all_to_all(cut_along(x, dim, devices), axis, 0, 0, tiled=True)
    return jnp.sum(blocks.astype(jnp.float32), axis=0)


def side_by_side(arrays, axis, dim, along):
    both = jnp.concatenate(arrays, axis=along)
    out, at, gathered = (sent_and_summed(both, axis, dim), 0, [])
    for a in arrays:
        gathered.append(lax.slice_in_dim(out, at, at + a.shape[along], axis=along))
        at += a.shape[along]
    return tuple(gathered)


def sent_to_all(x, axis):
    copies = jnp.broadcast_to(x, (lax.axis_size(axis), *x.shape))
    return lax.all_to_all(copies, axis, split_axis=0, concat_axis=0, tiled=True)


def of_everyone(x, axis):
    return sent_to_all(x, axis).sum(axis=0)


def normalize(inputs, gain_row):
    value_rows = inputs.astype(jnp.float32)
    inv_rms = lax.rsqrt(jnp.mean(value_rows * value_rows, axis=-1, keepdims=True) + EPSILON)
    unit_rows = value_rows * inv_rms
    return (unit_rows, inv_rms, (unit_rows * gain_row).astype(jnp.bfloat16))


def input_grads(inputs, grad_out, gain_row, w_value, w_out):
    unit_rows, inv_rms, normed = normalize(inputs, gain_row)
    grad_value = jnp.dot(grad_out, w_out, preferred_element_type=jnp.float32).astype(jnp.bfloat16)
    grad_normed = lax.dot_general(
        grad_value, w_value, (((1,), (1,)), ((), ())), preferred_element_type=jnp.float32
    )
    gain_term = jnp.sum(grad_normed * unit_rows, axis=0)
    grad_unit = grad_normed * gain_row
    grad_in = grad_out.astype(jnp.float32) + inv_rms * (
        grad_unit - unit_rows * jnp.mean(grad_unit * unit_rows, axis=-1, keepdims=True)
    )
    return (grad_in.astype(jnp.bfloat16), grad_value, normed, gain_term)


def arrivals(
    step_index, sent, section_count, section_index, micro_count, cotangent, local_saved, slot_order
):
    if step_index > 0:
        incoming = passed_along(sent, "section", -1)
    else:
        incoming = sent
    micro_index = step_index - (section_count - 1 - section_index)
    active_now = jnp.logical_and(micro_index >= 0, micro_index < micro_count)
    clipped = jnp.clip(micro_index, 0, micro_count - 1)
    top_grad = lax.dynamic_index_in_dim(cotangent, clipped, 0, keepdims=False)
    grad_out = jnp.where(section_index == section_count - 1, top_grad, incoming)
    slot_index = lax.dynamic_index_in_dim(slot_order, clipped, 0, keepdims=False)
    inputs = lax.dynamic_index_in_dim(local_saved, slot_index, 0, keepdims=False)
    return (active_now, clipped, grad_out, inputs)


def per_device(saved, cotangent, slot_table, gain, value_weight, out_weight):
    section_count = lax.axis_size("section")
    section_index = lax.axis_index("section")
    micro_count = slot_table.shape[1]
    local_saved = saved[0]
    slot_order = slot_table[0]
    gain_row = gain[0]
    w_value = value_weight[0]
    w_out = out_weight[0]
    token_rows = cotangent.shape[1]
    model_width = w_value.shape[0]
    inner_width = w_value.shape[1]
    sent = jnp.zeros((token_rows, model_width), jnp.bfloat16)
    gain_acc = jnp.zeros((model_width,), jnp.float32)
    out_stash = jnp.zeros((micro_count, token_rows, model_width), jnp.bfloat16)
    value_stash = jnp.zeros((micro_count, token_rows, inner_width), jnp.bfloat16)
    for step_index in range(micro_count + section_count - 1):
        active_now, clipped, grad_out, inputs = arrivals(
            step_index,
            sent,
            section_count,
            section_index,
            micro_count,
            cotangent,
            local_saved,
            slot_order,
        )

        def working(carried):
            grad_in, grad_value, normed, gain_term = input_grads(
                inputs, grad_out, gain_row, w_value, w_out
            )
            new_out = lax.dynamic_update_index_in_dim(carried[2], grad_out, clipped, 0)
            new_value = lax.dynamic_update_index_in_dim(carried[3], grad_value, clipped, 0)
            return (grad_in, carried[1] + gain_term, new_out, new_value)

        def resting(carried):
            return carried

        sent, gain_acc, out_stash, value_stash = lax.cond(
            active_now, working, resting, (sent, gain_acc, out_stash, value_stash)
        )
    ordered = jnp.take(local_saved, slot_order, axis=0).reshape(
        micro_count * token_rows, model_width
    )
    unit_all, inv_all, normed_all = normalize(ordered, gain_row)
    values_all = jnp.dot(normed_all, w_value, preferred_element_type=jnp.float32).astype(
        jnp.bfloat16
    )
    grads_all = out_stash.reshape(micro_count * token_rows, model_width)
    grad_values = value_stash.reshape(micro_count * token_rows, inner_width)
    value_acc = lax.dot_general(
        normed_all, grad_values, (((0,), (0,)), ((), ())), preferred_element_type=jnp.float32
    )
    out_acc = lax.dot_general(
        grads_all, values_all, (((0,), (0,)), ((), ())), preferred_element_type=jnp.float32
    )
    value_grad, out_grad = side_by_side(
        (value_acc.astype(jnp.bfloat16), out_acc.astype(jnp.bfloat16)), "seq", 0, 1
    )
    gain_total = of_everyone(gain_acc, "seq")
    return (value_grad[None], out_grad[None], gain_total[None])


def solution(mesh):
    in_specs = (
        P("section", None, "seq", None),
        P(None, "seq", None),
        P("section", None),
        P("section", None),
        P("section", None, None),
        P("section", None, None),
    )
    out_specs = (P("section", "seq", None), P("section", "seq", None), P("section", None))
    return jax.shard_map(
        per_device, mesh=mesh, in_specs=in_specs, out_specs=out_specs, check_vma=False
    )
```

profile of v0, /device:TPU:1, one launch (start us, length us, event | category | flops | bytes accessed | tf_op | source)
XLA Modules:
  0.0 403.9 jit_solution(3316975501780977007)
XLA Ops:
  0.7 1.5 constant_dynamic-slice_fusion.2
  9.7 1.1 select_bitcast_fusion
  10.8 3.0 dynamic-slice_bitcast_fusion
  13.8 3.2 conditional.6
  14.7 1.0 broadcast_in_dim.75
  15.7 1.3 broadcast_in_dim.74
  17.0 1.3 collective-permute-start
  18.3 29.7 %collective-permute-done = bf16[128,2304]{1,0:T(8,128)(2,1)} collective-permute-done((bf16[128,2304]{1,0:T(8,128)(2,1)}, bf16[128,2304]{1,0:T(8,128)(2,1)}, u32[]{:S(2)}, u32[]{:S(2)}) %collective-permute-start) | collective-permute-done | bytes 589856 | tf_op jit(solution)/shard_map/ppermute | solution.py:12
  48.0 1.1 bitcast_select_fusion.5
  49.2 1.3 collective-permute-start.1
  50.5 28.0 %collective-permute-done.1 = bf16[128,2304]{1,0:T(8,128)(2,1)} collective-permute-done((bf16[128,2304]{1,0:T(8,128)(2,1)}, bf16[128,2304]{1,0:T(8,128)(2,1)}, u32[]{:S(2)}, u32[]{:S(2)}) %collective-permute-start.1) | collective-permute-done | bytes 589856 | tf_op jit(solution)/shard_map/ppermute | solution.py:12
  78.5 1.1 bitcast_select_fusion.4
  79.6 1.3 collective-permute-start.2
  81.0 1.3 reduce.7
  83.3 32.9 %collective-permute-done.2 = bf16[128,2304]{1,0:T(8,128)(2,1)S(1)} collective-permute-done((bf16[128,2304]{1,0:T(8,128)(2,1)}, bf16[128,2304]{1,0:T(8,128)(2,1)S(1)}, u32[]{:S(2)}, u32[]{:S(2)}) %collective-permute-start.2) | collective-permute-done | bytes 589856 | tf_op jit(solution)/shard_map/ppermute | solution.py:12
  116.3 9.2 %conditional.9 = ((bf16[128,2304]{1,0:T(8,128)(2,1)}, f32[2304]{0:T(1024)S(1)}, bf16[3,128,2304]{2,1,0:T(8,128)(2,1)}, bf16[3,128,1024]{2,1,0:T(8,128)(2,1)})) conditional(s32[]{:T(128)} %convert_element_type.137, (bf16[128,2304]{1,0:T(8,128)(2,1)}, f32[2304]{0:T(1024)S(1)}, bf16[3,128,2304]{2,1,0:T(8,128)(2,1)}, ...), branch_computations={%region_16.17_spmd, %region_17.21_spmd} | conditional | flops 1213694080 | bytes 36254324 | solution.py:122
  117.6 4.0 bitcast_dynamic-update-slice_fusion.9
  121.5 0.9 bitcast_dynamic-update-slice_fusion.8
  122.4 1.8 fusion.41
  124.3 1.3 fusion.40
  125.5 1.3 collective-permute-start.3
  127.5 1.2 fusion.53
  128.7 16.7 %collective-permute-done.3 = bf16[128,2304]{1,0:T(8,128)(2,1)} collective-permute-done((bf16[128,2304]{1,0:T(8,128)(2,1)}, bf16[128,2304]{1,0:T(8,128)(2,1)}, u32[]{:S(2)}, u32[]{:S(2)}) %collective-permute-start.3) | collective-permute-done | bytes 589856 | tf_op jit(solution)/shard_map/ppermute | solution.py:12
  146.2 15.2 %conditional.10 = ((bf16[128,2304]{1,0:T(8,128)(2,1)}, f32[2304]{0:T(1024)S(1)}, bf16[3,128,2304]{2,1,0:T(8,128)(2,1)}, bf16[3,128,1024]{2,1,0:T(8,128)(2,1)})) conditional(s32[]{:T(128)} %convert_element_type.136, (bf16[128,2304]{1,0:T(8,128)(2,1)}, f32[2304]{0:T(1024)S(1)}, bf16[3,128,2304]{2,1,0:T(8,128)(2,1)}, ...), branch_computations={%region_21.22_spmd, %region_22.26_spmd.clone.clone} | conditional | flops 1213988992 | bytes 40127744 | solution.py:122
  146.2 1.2 constant_dynamic-slice_fusion.1
  149.4 2.6 bitcast_dynamic-update-slice_fusion.10
  152.7 1.3 reduce.6
  154.1 4.2 %bitcast_dynamic-update-slice_fusion.11 = (bf16[3,128,1024]{2,1,0:T(8,128)(2,1)}, bf16[128,1024]{1,0:T(8,128)(2,1)S(1)}) fusion(bf16[3,128,1024]{2,1,0:T(8,128)(2,1)} %get-tuple-element.434, s32[]{:T(128)S(6)} %select_n.153, bf16[128,2304]{1,0:T(8,128)(2,1)} %get-tuple-element.481, bf16[2304,1024]{1,0:T(8,128)(2,1)} %get-tuple-element.429), kind=kOutput, calls=%fused_computation.96 | convolution fusion | flops 604110848 | bytes 5832708 | tf_op jit(solution)/shard_map/cond/branch_1_fun/dot_general | solution.py:54
  158.3 1.9 fusion.51
  160.1 1.3 fusion.50
  161.4 1.3 collective-permute-start.4
  162.7 2.5 fusion.55
  165.2 8.3 %collective-permute-done.4 = bf16[128,2304]{1,0:T(8,128)(2,1)} collective-permute-done((bf16[128,2304]{1,0:T(8,128)(2,1)}, bf16[128,2304]{1,0:T(8,128)(2,1)}, u32[]{:S(2)}, u32[]{:S(2)}) %collective-permute-start.4) | collective-permute-done | bytes 589856 | tf_op jit(solution)/shard_map/ppermute | solution.py:12
  173.5 11.9 %conditional.11 = (f32[2304]{0:T(1024)S(1)}, bf16[3,128,1024]{2,1,0:T(8,128)(2,1)}, bf16[384,2304]{1,0:T(8,128)(2,1)}) conditional(s32[]{:T(128)} %convert_element_type.135, (f32[2304]{0:T(1024)S(1)}, bf16[3,128,1024]{2,1,0:T(8,128)(2,1)}, bf16[3,128,2304]{2,1,0:T(8,128)(2,1)}) %tuple.111, (bf16[3,128,2304]{2,1,0:T(8,128)(2,1)}, ...), branch_computations={%region_26.27_spmd, %region_27.30_spmd.clone.clone} | conditional | flops 1210744960 | bytes 30317764 | solution.py:122
  173.5 1.2 constant_dynamic-slice_fusion
  177.0 4.5 %bitcast_dynamic-update-slice_fusion.1 = (bf16[3,128,1024]{2,1,0:T(8,128)(2,1)}, bf16[128,1024]{1,0:T(8,128)(2,1)S(1)}) fusion(bf16[3,128,1024]{2,1,0:T(8,128)(2,1)} %get-tuple-element.456, s32[]{:T(128)S(6)} %select_n.156, bf16[2304,1024]{1,0:T(8,128)(2,1)} %get-tuple-element.453, pred[128,2304]{1,0:T(32,128)(4,1)} %get-tuple-element.449, ...), kind=kOutput, calls=%fused_computation.9 | convolution fusion | flops 604405760 | bytes 6717956 | tf_op jit(solution)/shard_map/cond/branch_1_fun/dot_general | solution.py:54
  181.4 2.3 bitcast_dynamic-update-slice_fusion
  183.7 1.7 fusion
  185.4 1.1 broadcast_in_dim.102
  186.5 15.2 %all-to-all-start.1 = ((f32[64,1,2304]{2,1,0:T(1,128)}), f32[64,1,2304]{2,1,0:T(1,128)S(1)}, u32[]{:S(2)}, u32[]{:S(2)}) async-start(f32[64,1,2304]{2,1,0:T(1,128)} %broadcast_in_dim.102), calls=%async_computation.1 | async-start | bytes 1179648 | tf_op jit(solution)/shard_map/all_to_all | solution.py:38
  201.8 8.5 %convolution_convert_fusion.6 = bf16[2304,1024]{0,1:T(8,128)(2,1)} fusion(bf16[384,2304]{1,0:T(8,128)(2,1)} %get-tuple-element.367, bf16[384,2304]{1,0:T(8,128)(2,1)S(1)} %bitcast.136, bf16[1,2304,1024]{2,1,0:T(8,128)(2,1)} %param.22), kind=kOutput, calls=%fused_computation.103 | convolution fusion | flops 3626631168 | bytes 12976128 | tf_op jit(solution)/shard_map/dot_general | solution.py:137
  210.3 3.9 bitcast_convert_fusion
  214.2 10.7 %pad_maximum_fusion = bf16[2304,2048]{0,1:T(8,128)(2,1)} fusion(bf16[2304,1024]{0,1:T(8,128)(2,1)S(1)} %copy-done.11, bf16[2304,1024]{0,1:T(8,128)(2,1)S(1)} %bitcast_convert_fusion), kind=kLoop, calls=%fused_computation.101 | loop fusion | flops 18874368 | bytes 18874368 | tf_op jit(solution)/shard_map/concatenate | solution.py:28
  224.9 12.8 %copy.15 = bf16[2304,2048]{1,0:T(8,128)(2,1)} copy(bf16[2304,2048]{0,1:T(8,128)(2,1)} %pad_maximum_fusion) | data formatting | bytes 18874368 | tf_op jit(solution)/shard_map/concatenate | solution.py:28
  237.7 13.1 %reshape.266 = bf16[64,36,2048]{2,1,0:T(8,128)(2,1)} reshape(bf16[2304,2048]{1,0:T(8,128)(2,1)} %copy.15) | data formatting | bytes 18874368 | tf_op jit(solution)/shard_map/reshape | solution.py:17
  250.8 9.0 %all-to-all-start = ((bf16[64,36,2048]{2,1,0:T(8,128)(2,1)}), bf16[64,36,2048]{2,1,0:T(8,128)(2,1)}, u32[]{:S(2)}, u32[]{:S(2)}) async-start(bf16[64,36,2048]{2,1,0:T(8,128)(2,1)} %reshape.266), calls=%async_computation | async-start | bytes 20971520 | tf_op jit(solution)/shard_map/all_to_all | solution.py:23
  260.7 135.2 %all-to-all-done = bf16[64,36,2048]{2,1,0:T(8,128)(2,1)} async-done(((bf16[64,36,2048]{2,1,0:T(8,128)(2,1)}), bf16[64,36,2048]{2,1,0:T(8,128)(2,1)}, u32[]{:S(2)}, u32[]{:S(2)}) %all-to-all-start) | async-done | bytes 9437216 | tf_op jit(solution)/shard_map/all_to_all | solution.py:23
  395.9 6.4 %convert_reduce_fusion = f32[36,2048]{1,0:T(8,128)S(1)} fusion(bf16[64,36,2048]{2,1,0:T(8,128)(2,1)} %all-to-all-done), kind=kLoop, calls=%fused_computation.100 | loop fusion | flops 9363456 | bytes 9732096 | tf_op jit(solution)/shard_map/reduce_sum | solution.py:24
  (58 shorter events, 8.1 us)
Async XLA Ops:
  13.8 34.2 %copy-start.6 = (bf16[3,128,2304]{2,1,0:T(8,128)(2,1)S(1)}, bf16[3,128,2304]{2,1,0:T(8,128)(2,1)}, u32[]{:S(2)}) copy-start(bf16[3,128,2304]{2,1,0:T(8,128)(2,1)} %param.19) | copy-start | bytes 5308420
  17.0 31.0 %collective-permute-start = (bf16[128,2304]{1,0:T(8,128)(2,1)}, bf16[128,2304]{1,0:T(8,128)(2,1)}, u32[]{:S(2)}, u32[]{:S(2)}) collective-permute-start(bf16[128,2304]{1,0:T(8,128)(2,1)} %get-tuple-element.337), channel_id=1, source_target_pairs={{64,0},{128,64},{192,128},{65,1},{129,65},{193,129},{66,2},{130,66... | collective-permute-start | bytes 1769480 | tf_op jit(solution)/shard_map/ppermute | solution.py:12
  49.2 29.3 %collective-permute-start.1 = (bf16[128,2304]{1,0:T(8,128)(2,1)}, bf16[128,2304]{1,0:T(8,128)(2,1)}, u32[]{:S(2)}, u32[]{:S(2)}) collective-permute-start(bf16[128,2304]{1,0:T(8,128)(2,1)} %get-tuple-element.341), channel_id=1, source_target_pairs={{64,0},{128,64},{192,128},{65,1},{129,65},{193,129},{66,2},{130,66... | collective-permute-start | bytes 1769480 | tf_op jit(solution)/shard_map/ppermute | solution.py:12
  79.6 2.7 copy-start.17
  79.6 36.6 %collective-permute-start.2 = (bf16[128,2304]{1,0:T(8,128)(2,1)}, bf16[128,2304]{1,0:T(8,128)(2,1)S(1)}, u32[]{:S(2)}, u32[]{:S(2)}) collective-permute-start(bf16[128,2304]{1,0:T(8,128)(2,1)} %get-tuple-element.345), channel_id=1, source_target_pairs={{64,0},{128,64},{192,128},{65,1},{129,65},{193,129},{66,2},{130,66... | collective-permute-start | bytes 1769480 | tf_op jit(solution)/shard_map/ppermute | solution.py:12
  116.3 10.5 %copy-start.20 = (s32[3]{0:T(128)S(1)}, s32[3]{0:T(128)}, u32[]{:S(2)}) copy-start(s32[3]{0:T(128)} %fusion.56) | copy-start | bytes 40
  116.3 10.6 %copy-start.5 = (bf16[1,3,128,2304]{3,2,1,0:T(8,128)(2,1)S(1)}, bf16[1,3,128,2304]{3,2,1,0:T(8,128)(2,1)}, u32[]{:S(2)}) copy-start(bf16[1,3,128,2304]{3,2,1,0:T(8,128)(2,1)} %param.18) | copy-start | bytes 5308420
  117.6 4.9 %copy-start.3 = (bf16[2304,1024]{1,0:T(8,128)(2,1)S(1)}, bf16[2304,1024]{1,0:T(8,128)(2,1)}, u32[]{:S(2)}) copy-start(bf16[2304,1024]{1,0:T(8,128)(2,1)} %get-tuple-element.282) | copy-start | bytes 14155780 | tf_op jit(solution)/shard_map/cond
  125.5 19.9 %collective-permute-start.3 = (bf16[128,2304]{1,0:T(8,128)(2,1)}, bf16[128,2304]{1,0:T(8,128)(2,1)}, u32[]{:S(2)}, u32[]{:S(2)}) collective-permute-start(bf16[128,2304]{1,0:T(8,128)(2,1)} %get-tuple-element.349), channel_id=1, source_target_pairs={{64,0},{128,64},{192,128},{65,1},{129,65},{193,129},{66,2},{130,66... | collective-permute-start | bytes 1769480 | tf_op jit(solution)/shard_map/ppermute | solution.py:12
  154.1 4.2 %copy-start.4 = (bf16[2304,1024]{1,0:T(8,128)(2,1)S(1)}, bf16[2304,1024]{1,0:T(8,128)(2,1)}, u32[]{:S(2)}) copy-start(bf16[2304,1024]{1,0:T(8,128)(2,1)} %get-tuple-element.430) | copy-start | bytes 14155780 | tf_op jit(solution)/shard_map/cond
  154.1 4.2 %copy-start.13 = (f32[2304]{0:T(1024)S(1)}, f32[2304]{0:T(1024)}, u32[]{:S(2)}) copy-start(f32[2304]{0:T(1024)} %reduce.6) | copy-start | bytes 27652 | tf_op jit(solution)/shard_map/cond
  154.1 4.2 %copy-start.18 = (f32[128]{0:T(128)S(1)}, f32[128]{0:T(128)}, u32[]{:S(2)}) copy-start(f32[128]{0:T(128)} %add_rsqrt_fusion.5) | copy-start | bytes 1540 | tf_op jit(solution)/shard_map/cond
  158.2 1.9 copy-start.9
  161.4 12.1 %collective-permute-start.4 = (bf16[128,2304]{1,0:T(8,128)(2,1)}, bf16[128,2304]{1,0:T(8,128)(2,1)}, u32[]{:S(2)}, u32[]{:S(2)}) collective-permute-start(bf16[128,2304]{1,0:T(8,128)(2,1)} %get-tuple-element.356), channel_id=1, source_target_pairs={{64,0},{128,64},{192,128},{65,1},{129,65},{193,129},{66,2},{130,66... | collective-permute-start | bytes 1769480 | tf_op jit(solution)/shard_map/ppermute | solution.py:12
  176.7 7.0 %slice-start = ((s8[4718592]{0:T(1024)(128)(4,1)}), s8[4194304]{0:T(1024)(128)(4,1)S(1)}, s32[]{:S(2)}) async-start(s8[4718592]{0:T(1024)(128)(4,1)} %bitcast.133), calls=%async_computation.2 | async-start | bytes 8388608 | tf_op jit(solution)/shard_map/cond
  176.9 4.5 %copy-start.10 = (pred[128,2304]{1,0:T(32,128)(4,1)S(1)}, pred[128,2304]{1,0:T(32,128)(4,1)}, u32[]{:S(2)}) copy-start(pred[128,2304]{1,0:T(32,128)(4,1)} %get-tuple-element.449) | copy-start | bytes 884740 | tf_op jit(solution)/shard_map/cond
  177.0 6.7 %slice-start.1 = ((s8[4718592]{0:T(1024)(128)(4,1)}), s8[524288]{0:T(1024)(128)(4,1)S(1)}, s32[]{:S(2)}) async-start(s8[4718592]{0:T(1024)(128)(4,1)} %bitcast.133), calls=%async_computation.3 | async-start | bytes 1048576 | tf_op jit(solution)/shard_map/cond
  185.4 16.4 %copy-start.12 = (bf16[3,128,2304]{2,1,0:T(8,128)(2,1)S(1)}, bf16[3,128,2304]{2,1,0:T(8,128)(2,1)}, u32[]{:S(2)}) copy-start(bf16[3,128,2304]{2,1,0:T(8,128)(2,1)} %fusion.55) | copy-start | bytes 5308420
  186.5 64.2 %all-to-all-start.1 = ((f32[64,1,2304]{2,1,0:T(1,128)}), f32[64,1,2304]{2,1,0:T(1,128)S(1)}, u32[]{:S(2)}, u32[]{:S(2)}) async-start(f32[64,1,2304]{2,1,0:T(1,128)} %broadcast_in_dim.102), calls=%async_computation.1 | async-start | bytes 1179648 | tf_op jit(solution)/shard_map/all_to_all | solution.py:38
  210.3 3.9 copy-start.11
  250.8 145.2 %all-to-all-start = ((bf16[64,36,2048]{2,1,0:T(8,128)(2,1)}), bf16[64,36,2048]{2,1,0:T(8,128)(2,1)}, u32[]{:S(2)}, u32[]{:S(2)}) async-start(bf16[64,36,2048]{2,1,0:T(8,128)(2,1)} %reshape.266), calls=%async_computation | async-start | bytes 20971520 | tf_op jit(solution)/shard_map/all_to_all | solution.py:23
where the time goes:
time: 406 us; the launch traced here: 404 us
  waiting for transfers between devices  251 us (62%)
  local copies, waits for them, and re-layouts  41.7 us (10%)
  other arithmetic  37.7 us (9%)
  starting transfers between devices  30.7 us (8%)
  matrix products  30.4 us (7%)
  between operations  8.49 us (2%)
  loops' own time  4.21 us (1%)
    all_to_all x1, waiting for transfers between devices, sent_and_summed(): blocks = lax.all_to_all(cut_along(x, dim, devices), axis, 0, 0, tiled=True)  135 us
    ppermute x5, waiting for transfers between devices, passed_along(): lax.ppermute(value, axis, [(source, source + steps) for source in range(f...  116 us
    all_to_all x1, starting transfers between devices, sent_to_all(): return lax.all_to_all(copies, axis, split_axis=0, concat_axis=0, tiled=True)  15.2 us
    reshape x1, local copies, waits for them, and re-layouts, cut_along(): x.reshape(*shape[:dim], devices, shape[dim] // devices, *shape[dim + 1:])  13.1 us
    concatenate x1, local copies, waits for them, and re-layouts, side_by_side(): both = jnp.concatenate(arrays, axis=along)  12.8 us
    dot_general x3, matrix products, input_grads(): jnp.dot(grad_out, w_out, preferred_element_type=jnp.float32)  12.6 us
    concatenate x1, other arithmetic, side_by_side(): both = jnp.concatenate(arrays, axis=along)  10.7 us
    all_to_all x1, starting transfers between devices, sent_and_summed(): blocks = lax.all_to_all(cut_along(x, dim, devices), axis, 0, 0, tiled=True)  9.01 us
  transfers between devices with their start and end apart: 7, of which 6 were waited for; matrix products, arithmetic and copies ran while one was open for 14% of the time, Pallas kernels for 0%

commit v1 on v0

v1 whole, which is shorter than its diff:
```python
import functools

import jax
import jax.numpy as jnp
from jax import lax
from jax.experimental import pallas as pl
from jax.experimental.pallas import tpu as pltpu
from jax.sharding import PartitionSpec as P

EPSILON = 1e-06
MESH = pl.DeviceIdType.MESH
F32 = jnp.float32
BF16 = jnp.bfloat16

CHUNK = 32
NY, NZ, NX, NC = 4, 2, 4, 2
LANES = 128


def kernel(
    sections,
    slot_ref,
    gain_ref,
    x_hbm,
    cot_hbm,
    wv_hbm,
    wo_hbm,
    ov_ref,
    oo_ref,
    og_ref,
    xb,
    gb,
    wv,
    wo,
    gout,
    ll,
    rr,
    lo,
    ro,
    acc,
    gacc,
    st1,
    r1,
    st2,
    r2,
    st3,
    r3,
    fin,
    give,
    take,
    gc,
    gx,
    gy,
    gz,
    load_sem,
    g_send,
    g_recv,
    l_send,
    l_recv,
    rr_send,
    rr_recv,
    s1_send,
    s1_recv,
    s2_send,
    s2_recv,
    s3_send,
    s3_recv,
    f_send,
    f_recv,
    gc_send,
    gc_recv,
    gx_send,
    gx_recv,
    gy_send,
    gy_recv,
    gz_send,
    gz_recv,
):
    micro, tokens, width = xb.shape
    inner = wv.shape[1]
    per_micro = tokens // CHUNK
    chunks = micro * per_micro
    rows = width // (NY * NZ * NX)
    half = rows // NC

    sec = lax.axis_index("section")
    q = lax.axis_index("seq")
    core = lax.rem(q, NC)
    xi = lax.rem(q // NC, NX)
    zi = lax.rem(q // (NC * NX), NZ)
    yi = q // (NC * NX * NZ)

    def at(y, z, x, c):
        return (sec, ((y * NZ + z) * NX + x) * NC + c)

    partner = at(yi, zi, xi, 1 - core)
    x_peer = [at(yi, zi, lax.rem(xi + d, NX), core) for d in range(NX)]
    y_peer = [at(lax.rem(yi + d, NY), zi, xi, core) for d in range(NY)]
    z_peer = at(yi, 1 - zi, xi, core)
    above = (lax.rem(sec + 1, sections), q)
    below = (lax.rem(sec + sections - 1, sections), q)

    wo_load = pltpu.make_async_copy(wo_hbm, wo, load_sem.at[0])
    x_load = pltpu.make_async_copy(x_hbm, xb, load_sem.at[1])
    wv_load = pltpu.make_async_copy(wv_hbm, wv, load_sem.at[2])

    def chunk_of(k):
        return k // per_micro, pl.ds(pl.multiple_of(lax.rem(k, per_micro) * CHUNK, CHUNK), CHUNK)

    def top_load(k):
        m, at_rows = chunk_of(k)
        return pltpu.make_async_copy(cot_hbm.at[m, at_rows], gb.at[m, at_rows], g_recv.at[k])

    def down(k):
        m, at_rows = chunk_of(k)
        return pltpu.make_async_remote_copy(
            src_ref=gout.at[m, at_rows],
            dst_ref=gb.at[m, at_rows],
            send_sem=g_send.at[k],
            recv_sem=g_recv.at[k],
            device_id=below,
            device_id_type=MESH,
        )

    is_top = sec == sections - 1

    @pl.when(is_top)
    def _():
        @pl.loop(0, chunks)
        def _(k):
            top_load(k).start()

    wo_load.start()
    x_load.start()
    wv_load.start()

    barrier = pltpu.get_barrier_semaphore()
    peers = [above, below, partner, z_peer] + x_peer[1:] + y_peer[1:]
    for peer in peers:
        pl.semaphore_signal(barrier, inc=1, device_id=peer, device_id_type=MESH)
    pl.semaphore_wait(barrier, len(peers))

    wo_load.wait()
    x_load.wait()
    wv_load.wait()
    gacc[...] = jnp.zeros_like(gacc)

    def left_copy(k):
        m, at_rows = chunk_of(k)
        far = pl.ds(pl.multiple_of(tokens + lax.rem(k, per_micro) * CHUNK, CHUNK), CHUNK)
        return pltpu.make_async_remote_copy(
            src_ref=lo.at[m, at_rows],
            dst_ref=ll.at[m, far],
            send_sem=l_send.at[k],
            recv_sem=l_recv.at[k],
            device_id=partner,
            device_id_type=MESH,
        )

    def right_copy(k):
        m, at_rows = chunk_of(k)
        far = pl.ds(pl.multiple_of(tokens + lax.rem(k, per_micro) * CHUNK, CHUNK), CHUNK)
        return pltpu.make_async_remote_copy(
            src_ref=ro.at[m, at_rows],
            dst_ref=rr.at[m, far],
            send_sem=rr_send.at[k],
            recv_sem=rr_recv.at[k],
            device_id=partner,
            device_id_type=MESH,
        )

    blocks = 9
    wide = width // blocks

    def accumulate(m, first):
        @pl.loop(0, per_micro)
        def _(j):
            left_copy(m * per_micro + j).wait_recv()
            right_copy(m * per_micro + j).wait_recv()

        @pl.loop(0, blocks)
        def _(b):
            cols = pl.ds(pl.multiple_of(b * wide, wide), wide)
            term = lax.dot_general(
                ll[m, :, cols], rr[m], (((0,), (0,)), ((), ())), preferred_element_type=F32
            )
            if first:
                acc[cols, :] = term
            else:
                acc[cols, :] += term

    @pl.loop(0, chunks)
    def _(k):
        m, at_rows = chunk_of(k)

        @pl.when(is_top)
        def _():
            top_load(k).wait()

        @pl.when(jnp.logical_not(is_top))
        def _():
            down(k).wait_recv()

        g = gb[m, at_rows, :]
        slot = slot_ref[0, m]
        x = xb[slot, at_rows, :].astype(F32)
        gain = gain_ref[...]
        inv = lax.rsqrt(jnp.mean(x * x, axis=-1, keepdims=True) + EPSILON)
        unit = x * inv
        n = (unit * gain).astype(BF16)
        gv = jnp.dot(g, wo[...], preferred_element_type=F32).astype(BF16)
        gn = lax.dot_general(gv, wv[...], (((1,), (1,)), ((), ())), preferred_element_type=F32)
        gu_terms = gn * unit
        gu = gn * gain
        centre = jnp.mean(gu * unit, axis=-1, keepdims=True)
        gout[m, at_rows, :] = (g.astype(F32) + inv * (gu - unit * centre)).astype(BF16)
        part = gu_terms[0:8]
        for j in range(1, CHUNK // 8):
            part = part + gu_terms[8 * j : 8 * j + 8]
        gacc[...] += part

        @pl.when(sec > 0)
        def _():
            down(k).start()

        v = jnp.dot(n, wv[...], preferred_element_type=F32).astype(BF16)
        ll[m, at_rows, :] = jnp.where(core == 0, n, g)
        lo[m, at_rows, :] = jnp.where(core == 0, g, n)
        rr[m, at_rows, :] = jnp.where(core == 0, gv, v)
        ro[m, at_rows, :] = jnp.where(core == 0, v, gv)
        left_copy(k).start()
        right_copy(k).start()

        @pl.when(k == per_micro + 1)
        def _():
            accumulate(0, True)

        if micro > 2:

            @pl.when(jnp.logical_and(lax.rem(k, per_micro) == 1, k > 2 * per_micro))
            def _():
                accumulate(m - 1, False)

    own_gain = jnp.sum(gacc[...], axis=0, keepdims=True)
    gc[core] = own_gain
    gc_copy = pltpu.make_async_remote_copy(
        src_ref=gc.at[core],
        dst_ref=gc.at[core],
        send_sem=gc_send,
        recv_sem=gc_recv,
        device_id=partner,
        device_id_type=MESH,
    )
    gc_copy.start()

    accumulate(micro - 1, False)

    def pieces(y, z, x):
        p = (y * NZ + z) * NX + x
        return pl.ds(pl.multiple_of(p * rows, 8), rows)

    def stage_first(part, dest, hs):
        lane0 = part * 2 * LANES

        @pl.loop(0, NY * NZ)
        def _(j):
            other, z = j // NZ, lax.rem(j, NZ)
            block_rows = pieces(other, z, dest) if part == 0 else pieces(dest, z, other)
            for h in hs:
                lane = lane0 + h * LANES
                top = acc[block_rows, lane : lane + LANES]
                bottom = acc[block_rows, inner // 2 + lane : inner // 2 + lane + LANES]
                st1[part, dest, h, j] = jnp.concatenate([top, bottom], axis=0).astype(BF16)

    def ring_copy(st, r, send, recv, part, slot, src, h, peer):
        return pltpu.make_async_remote_copy(
            src_ref=st.at[part, src, h],
            dst_ref=r.at[part, slot],
            send_sem=send.at[part, slot],
            recv_sem=recv.at[part, slot],
            device_id=peer,
            device_id_type=MESH,
        )

    def ring(st, r, send, recv, part, mine, n, peer):
        plus, minus, across = lax.rem(mine + 1, n), lax.rem(mine + 3, n), lax.rem(mine + 2, n)
        to_plus, to_minus = peer[1], peer[3]
        copy = functools.partial(ring_copy, st, r, send, recv, part)
        return [
            copy(0, across, 0, to_plus),
            copy(1, across, 1, to_minus),
            copy(2, plus, 1, to_plus),
            copy(3, minus, 0, to_minus),
            copy(4, plus, 0, to_plus),
            copy(5, minus, 1, to_minus),
        ]

    dims = [(xi, NX, x_peer), (yi, NY, y_peer)]
    first = [ring(st1, r1, s1_send, s1_recv, part, *dims[part]) for part in range(2)]
    second = [ring(st2, r2, s2_send, s2_recv, part, *dims[1 - part]) for part in range(2)]

    def neighbours(i, n):
        return lax.rem(i + 1, n), lax.rem(i + 3, n), lax.rem(i + 2, n)

    for part in range(2):
        plus, minus, across = neighbours(*dims[part][:2])
        stage_first(part, across, (0, 1))
        first[part][0].start()
        first[part][1].start()
    for part in range(2):
        plus, minus, across = neighbours(*dims[part][:2])
        stage_first(part, plus, (1,))
        first[part][2].start()
        stage_first(part, minus, (0,))
        first[part][3].start()

    gc_copy.wait_recv()
    gx[xi] = gc[0] + gc[1]
    gx_copies = []
    for d in range(1, NX):
        copy = pltpu.make_async_remote_copy(
            src_ref=gx.at[xi],
            dst_ref=gx.at[xi],
            send_sem=gx_send.at[d],
            recv_sem=gx_recv.at[xi],
            device_id=x_peer[d],
            device_id_type=MESH,
        )
        copy.start()
        gx_copies.append(copy)

    for part in range(2):
        plus, minus, across = neighbours(*dims[part][:2])
        stage_first(part, plus, (0,))
        stage_first(part, minus, (1,))
        stage_first(part, dims[part][0], (0, 1))

    def hop(st, r, copies, part, mine, n, loops):
        plus, minus, across = neighbours(mine, n)
        for slot, dest, h, onward in ((0, plus, 0, 4), (1, minus, 1, 5)):
            copies[slot].wait_recv()

            @pl.loop(0, loops)
            def _(j):
                st[part, dest, h, j] = (
                    st[part, dest, h, j].astype(F32) + r[part, slot, j].astype(F32)
                ).astype(BF16)

            copies[onward].start()

    for part in range(2):
        hop(st1, r1, first[part], part, *dims[part][:2], NY * NZ)

    def gathered(buf, recv, mine, n):
        for d in range(1, n):
            j = lax.rem(mine + d, n)
            pltpu.make_async_remote_copy(
                src_ref=buf.at[j],
                dst_ref=buf.at[j],
                send_sem=gx_send.at[0],
                recv_sem=recv.at[j],
                device_id=partner,
                device_id_type=MESH,
            ).wait_recv()
        total = buf[0]
        for j in range(1, n):
            total = total + buf[j]
        return total

    gy[yi] = gathered(gx, gx_recv, xi, NX)
    gy_copies = []
    for d in range(1, NY):
        copy = pltpu.make_async_remote_copy(
            src_ref=gy.at[yi],
            dst_ref=gy.at[yi],
            send_sem=gy_send.at[d],
            recv_sem=gy_recv.at[yi],
            device_id=y_peer[d],
            device_id_type=MESH,
        )
        copy.start()
        gy_copies.append(copy)

    for part in range(2):
        mine = dims[part][0]
        for h, slots in ((0, (3, 4)), (1, (2, 5))):
            for slot in slots:
                first[part][slot].wait_recv()

            @pl.loop(0, NY * NZ)
            def _(j):
                total = (
                    st1[part, mine, h, j].astype(F32)
                    + r1[part, slots[0], j].astype(F32)
                    + r1[part, slots[1], j].astype(F32)
                )
                st2[part, j // NZ, h, lax.rem(j, NZ)] = total.astype(BF16)

        for j in range(4):
            second[part][j].start()

    gz[zi] = gathered(gy, gy_recv, yi, NY)
    gz_copy = pltpu.make_async_remote_copy(
        src_ref=gz.at[zi],
        dst_ref=gz.at[zi],
        send_sem=gz_send,
        recv_sem=gz_recv,
        device_id=z_peer,
        device_id_type=MESH,
    )
    gz_copy.start()

    for part in range(2):
        hop(st2, r2, second[part], part, *dims[1 - part][:2], NZ)

    def z_copy(part):
        return pltpu.make_async_remote_copy(
            src_ref=st3.at[part, 1 - zi],
            dst_ref=r3.at[part],
            send_sem=s3_send.at[part],
            recv_sem=s3_recv.at[part],
            device_id=z_peer,
            device_id_type=MESH,
        )

    for part in range(2):
        mine = dims[1 - part][0]
        for h, slots in ((0, (3, 4)), (1, (2, 5))):
            for slot in slots:
                second[part][slot].wait_recv()
            for z in range(NZ):
                total = (
                    st2[part, mine, h, z].astype(F32)
                    + r2[part, slots[0], z].astype(F32)
                    + r2[part, slots[1], z].astype(F32)
                )
                st3[part, z, h] = total.astype(BF16)
        z_copy(part).start()

    for part in range(2):
        z_copy(part).wait_recv()
        for h in range(2):
            total = st3[part, zi, h].astype(F32) + r3[part, h].astype(F32)
            lane = (part * 2 + h) * LANES
            fin[:, lane : lane + LANES] = total[:rows]
            fin[:, inner // 2 + lane : inner // 2 + lane + LANES] = total[rows:]

    low, high = fin[0:half, :], fin[half:rows, :]
    give[...] = jnp.where(core == 0, high, low)
    swap = pltpu.make_async_remote_copy(
        src_ref=give,
        dst_ref=take,
        send_sem=f_send,
        recv_sem=f_recv,
        device_id=partner,
        device_id_type=MESH,
    )
    swap.start()
    keep = jnp.where(core == 0, low, high)
    gz_copy.wait_recv()
    og_ref[...] = gz[0] + gz[1]
    swap.wait_recv()
    other = take[...]
    ov_ref[...] = jnp.where(core == 0, keep, other)
    oo_ref[...] = jnp.where(core == 0, other, keep)

    @pl.when(sec > 0)
    def _():
        @pl.loop(0, chunks)
        def _(k):
            down(k).wait_send()

    @pl.loop(0, chunks)
    def _(k):
        left_copy(k).wait_send()
        right_copy(k).wait_send()

    for part in range(2):
        for j in range(6):
            first[part][j].wait_send()
            second[part][j].wait_send()
        z_copy(part).wait_send()
    for copy in [gc_copy, gz_copy, swap] + gx_copies + gy_copies:
        copy.wait_send()


def per_device(sections, saved, cotangent, slot_table, gain, value_weight, out_weight):
    micro, tokens, width = cotangent.shape
    inner = value_weight.shape[2]
    rows = width // (NY * NZ * NX)
    chunks = micro * (tokens // CHUNK)
    unit = (2 * rows, LANES)
    n1 = NY * NZ
    dma = pltpu.SemaphoreType.DMA
    hbm = pl.BlockSpec(memory_space=pl.ANY)
    vmem = pl.BlockSpec(memory_space=pltpu.VMEM)
    ov, oo, og = pl.pallas_call(
        functools.partial(kernel, sections),
        out_shape=(
            jax.ShapeDtypeStruct((rows // NC, inner), F32),
            jax.ShapeDtypeStruct((rows // NC, inner), F32),
            jax.ShapeDtypeStruct((1, width), F32),
        ),
        in_specs=[pl.BlockSpec(memory_space=pltpu.SMEM), vmem, hbm, hbm, hbm, hbm],
        out_specs=(vmem, vmem, vmem),
        scratch_shapes=[
            pltpu.VMEM((micro, tokens, width), BF16),
            pltpu.VMEM((micro, tokens, width), BF16),
            pltpu.VMEM((width, inner), BF16),
            pltpu.VMEM((width, inner), BF16),
            pltpu.VMEM((micro, tokens, width), BF16),
            pltpu.VMEM((micro, 2 * tokens, width), BF16),
            pltpu.VMEM((micro, 2 * tokens, inner), BF16),
            pltpu.VMEM((micro, tokens, width), BF16),
            pltpu.VMEM((micro, tokens, inner), BF16),
            pltpu.VMEM((width, inner), F32),
            pltpu.VMEM((8, width), F32),
            pltpu.VMEM((2, 4, 2, n1) + unit, BF16),
            pltpu.VMEM((2, 6, n1) + unit, BF16),
            pltpu.VMEM((2, 4, 2, NZ) + unit, BF16),
            pltpu.VMEM((2, 6, NZ) + unit, BF16),
            pltpu.VMEM((2, NZ, 2) + unit, BF16),
            pltpu.VMEM((2, 2) + unit, BF16),
            pltpu.VMEM((rows, inner), F32),
            pltpu.VMEM((rows // NC, inner), F32),
            pltpu.VMEM((rows // NC, inner), F32),
            pltpu.VMEM((NC, 1, width), F32),
            pltpu.VMEM((NX, 1, width), F32),
            pltpu.VMEM((NY, 1, width), F32),
            pltpu.VMEM((NZ, 1, width), F32),
            dma((3,)),
            dma((chunks,)),
            dma((chunks,)),
            dma((chunks,)),
            dma((chunks,)),
            dma((chunks,)),
            dma((chunks,)),
            dma((2, 6)),
            dma((2, 6)),
            dma((2, 6)),
            dma((2, 6)),
            dma((2,)),
            dma((2,)),
            dma,
            dma,
            dma,
            dma,
            dma((NX,)),
            dma((NX,)),
            dma((NY,)),
            dma((NY,)),
            dma,
            dma,
        ],
        compiler_params=pltpu.CompilerParams(
            collective_id=0, has_side_effects=True, vmem_limit_bytes=62 * 1024 * 1024
        ),
    )(slot_table, gain, saved[0], cotangent, value_weight[0], out_weight[0])
    return (ov[None], oo[None], og)


def solution(mesh):
    in_specs = (
        P("section", None, "seq", None),
        P(None, "seq", None),
        P("section", None),
        P("section", None),
        P("section", None, None),
        P("section", None, None),
    )
    out_specs = (P("section", "seq", None), P("section", "seq", None), P("section", None))
    return jax.shard_map(
        functools.partial(per_device, mesh.shape["section"]),
        mesh=mesh,
        in_specs=in_specs,
        out_specs=out_specs,
        check_vma=False,
    )
```

time: 406 us -> 178 us (0.44)
  waiting for transfers between devices: 251 us -> 0 us
  Pallas kernels: 0 us -> 170 us
  other arithmetic: 37.7 us -> 0 us
  local copies, waits for them, and re-layouts: 41.7 us -> 4.75 us
  starting transfers between devices: 30.7 us -> 0 us
  matrix products: 30.4 us -> 0 us
  between operations: 8.49 us -> 0.64 us
  loops' own time: 4.21 us -> 0 us
    pallas_call x0 -> x1, Pallas kernels: none -> 170 us  [per_device(): pl.pallas_call(functools.partial(kernel, sections), out_shape=(jax.ShapeD...]
    all_to_all x2 -> x0, waiting for transfers between devices: 135 us -> none  [the longest x1 135 us: sent_and_summed(): blocks = lax.all_to_all(cut_along(x, dim, devices), axis, 0, 0, tiled=True)]
    ppermute x5 -> x0, waiting for transfers between devices: 116 us -> none  [passed_along(): lax.ppermute(value, axis, [(source, source + steps) for source in range(f...]
    dot_general x8 -> x0, matrix products: 30.4 us -> none  [the longest x3 12.6 us: input_grads(): jnp.dot(grad_out, w_out, preferred_element_type=jnp.float32)]
    all_to_all x2 -> x0, starting transfers between devices: 24.2 us -> none  [the longest x1 15.2 us: sent_to_all(): return lax.all_to_all(copies, axis, split_axis=0, concat_axis=0, tiled=True)]
    reshape x1 -> x0, local copies, waits for them, and re-layouts: 13.1 us -> none  [cut_along(): x.reshape(*shape[:dim], devices, shape[dim] // devices, *shape[dim + 1:])]
    concatenate x1 -> x0, local copies, waits for them, and re-layouts: 12.8 us -> none  [side_by_side(): both = jnp.concatenate(arrays, axis=along)]
    concatenate x1 -> x0, other arithmetic: 10.7 us -> none  [side_by_side(): both = jnp.concatenate(arrays, axis=along)]
  transfers between devices with their start and end apart: 7 -> 0, of which waited for: 6 -> 0; matrix products, arithmetic and copies ran while one was open for 14% -> 0% of each run, Pallas kernels for 0% -> 0%
where the time goes in v1:
time: 178 us; the launch traced here: 175 us
  Pallas kernels  170 us (96%)
  local copies, waits for them, and re-layouts  4.75 us (3%)
    pallas_call x1, Pallas kernels, per_device(): pl.pallas_call(functools.partial(kernel, sections), out_shape=(jax.ShapeD...  170 us
    unnamed x3, local copies, waits for them, and re-layouts  4.75 us

profile of v1, /device:TPU:1, one launch (start us, length us, event | category | flops | bytes accessed | tf_op | source)
XLA Modules:
  0.0 175.5 jit_solution(6365153603717187241)
XLA Ops:
  0.6 170.1 %shard_map.85 = (f32[36,1024]{1,0:T(8,128)}, f32[36,1024]{1,0:T(8,128)}, f32[1,2304]{1,0:T(1,128)}) custom-call(s32[1,3]{1,0:T(1,128)} %slot_ref.1, f32[1,2304]{1,0:T(1,128)} %gain_ref.1, bf16[3,128,2304]{2,1,0:T(8,128)(2,1)} %bitcast.7, bf16[3,128,2304]{2,1,0:T(8,128)(2,1)} %cot_hbm.1, bf16[2304,1024]{1,0:T(8,128)(2,1)} %bitcast.5, bf16[2304,1024]{1,0:T(8,128)(2,1)} %bitcast.6), custom_call_target="tpu_custom_call" | custom-call | tf_op jit(solution)/shard_map/pallas_call | solution.py:497
  170.7 1.7 copy.9
  172.4 1.7 copy.10
  174.2 1.3 copy.12

commit v2 on v1

--- a/solution.py
+++ b/solution.py
@@ -32,6 +32,9 @@
     gb,
     wv,
     wo,
+    wvt,
+    nb,
+    vb,
     gout,
     ll,
     rr,
@@ -123,6 +126,7 @@
         )
 
     is_top = sec == sections - 1
+    wv_load.start()
 
     @pl.when(is_top)
     def _():
@@ -132,18 +136,49 @@
 
     wo_load.start()
     x_load.start()
-    wv_load.start()
 
     barrier = pltpu.get_barrier_semaphore()
     peers = [above, below, partner, z_peer] + x_peer[1:] + y_peer[1:]
     for peer in peers:
         pl.semaphore_signal(barrier, inc=1, device_id=peer, device_id_type=MESH)
-    pl.semaphore_wait(barrier, len(peers))
-
-    wo_load.wait()
-    x_load.wait()
-    wv_load.wait()
-    gacc[...] = jnp.zeros_like(gacc)
+
+    gain = gain_ref[...]
+
+    def normed(x):
+        inv = lax.rsqrt(jnp.mean(x * x, axis=-1, keepdims=True) + EPSILON)
+        unit = x * inv
+        return inv, unit, (unit * gain).astype(BF16)
+
+    with jax.named_scope("loads"):
+        gacc[...] = jnp.zeros_like(gacc)
+        wv_load.wait()
+
+        @pl.loop(0, width // 256)
+        def _(b):
+            at_cols = pl.ds(pl.multiple_of(b * 256, 256), 256)
+            wvt[:, at_cols] = wv[at_cols, :].T
+
+        wo_load.wait()
+        x_load.wait()
+
+    with jax.named_scope("barrier"):
+        pl.semaphore_wait(barrier, len(peers))
+
+    with jax.named_scope("prepare"):
+
+        @pl.when(jnp.logical_not(is_top))
+        def _():
+            @pl.loop(0, micro)
+            def _(m):
+                slot = slot_ref[0, m]
+
+                @pl.loop(0, per_micro)
+                def _(j):
+                    at_rows = pl.ds(pl.multiple_of(j * CHUNK, CHUNK), CHUNK)
+                    _, _, n = normed(xb[slot, at_rows, :].astype(F32))
+                    nb[m, at_rows, :] = n
+
+                vb[m] = jnp.dot(nb[m], wv[...], preferred_element_type=F32).astype(BF16)
 
     def left_copy(k):
         m, at_rows = chunk_of(k)
@@ -169,77 +204,87 @@
             device_id_type=MESH,
         )
 
-    blocks = 9
-    wide = width // blocks
-
-    def accumulate(m, first):
+    wide = 256
+
+    def received(m):
         @pl.loop(0, per_micro)
         def _(j):
             left_copy(m * per_micro + j).wait_recv()
             right_copy(m * per_micro + j).wait_recv()
 
-        @pl.loop(0, blocks)
-        def _(b):
-            cols = pl.ds(pl.multiple_of(b * wide, wide), wide)
-            term = lax.dot_general(
-                ll[m, :, cols], rr[m], (((0,), (0,)), ((), ())), preferred_element_type=F32
-            )
-            if first:
-                acc[cols, :] = term
-            else:
-                acc[cols, :] += term
+    def add_columns(m, at_cols, first):
+        term = lax.dot_general(
+            ll[m], rr[m, :, at_cols], (((0,), (0,)), ((), ())), preferred_element_type=F32
+        )
+        if first:
+            acc[:, at_cols] = term
+        else:
+            acc[:, at_cols] += term
+
+    def accumulate(m, first):
+        received(m)
+
+        @pl.loop(0, inner // wide)
+        def _(c):
+            add_columns(m, pl.ds(pl.multiple_of(c * wide, wide), wide), first)
 
     @pl.loop(0, chunks)
     def _(k):
         m, at_rows = chunk_of(k)
 
-        @pl.when(is_top)
-        def _():
-            top_load(k).wait()
-
-        @pl.when(jnp.logical_not(is_top))
-        def _():
-            down(k).wait_recv()
-
-        g = gb[m, at_rows, :]
-        slot = slot_ref[0, m]
-        x = xb[slot, at_rows, :].astype(F32)
-        gain = gain_ref[...]
-        inv = lax.rsqrt(jnp.mean(x * x, axis=-1, keepdims=True) + EPSILON)
-        unit = x * inv
-        n = (unit * gain).astype(BF16)
-        gv = jnp.dot(g, wo[...], preferred_element_type=F32).astype(BF16)
-        gn = lax.dot_general(gv, wv[...], (((1,), (1,)), ((), ())), preferred_element_type=F32)
-        gu_terms = gn * unit
-        gu = gn * gain
-        centre = jnp.mean(gu * unit, axis=-1, keepdims=True)
-        gout[m, at_rows, :] = (g.astype(F32) + inv * (gu - unit * centre)).astype(BF16)
-        part = gu_terms[0:8]
-        for j in range(1, CHUNK // 8):
-            part = part + gu_terms[8 * j : 8 * j + 8]
-        gacc[...] += part
+        with jax.named_scope("gwait"):
+
+            @pl.when(is_top)
+            def _():
+                top_load(k).wait()
+
+            @pl.when(jnp.logical_not(is_top))
+            def _():
+                down(k).wait_recv()
+
+        with jax.named_scope("main"):
+            g = gb[m, at_rows, :]
+            inv, unit, n = normed(xb[slot_ref[0, m], at_rows, :].astype(F32))
+            gv = jnp.dot(g, wo[...], preferred_element_type=F32).astype(BF16)
+            gn = jnp.dot(gv, wvt[...], preferred_element_type=F32)
+            gu_terms = gn * unit
+            gu = gn * gain
+            centre = jnp.mean(gu * unit, axis=-1, keepdims=True)
+            gout[m, at_rows, :] = (g.astype(F32) + inv * (gu - unit * centre)).astype(BF16)
+            part = gu_terms[0:8]
+            for j in range(1, CHUNK // 8):
+                part = part + gu_terms[8 * j : 8 * j + 8]
+            gacc[...] += part
 
         @pl.when(sec > 0)
         def _():
             down(k).start()
 
-        v = jnp.dot(n, wv[...], preferred_element_type=F32).astype(BF16)
-        ll[m, at_rows, :] = jnp.where(core == 0, n, g)
-        lo[m, at_rows, :] = jnp.where(core == 0, g, n)
-        rr[m, at_rows, :] = jnp.where(core == 0, gv, v)
-        ro[m, at_rows, :] = jnp.where(core == 0, v, gv)
-        left_copy(k).start()
-        right_copy(k).start()
+        with jax.named_scope("share"):
+
+            @pl.when(is_top)
+            def _():
+                vb[m, at_rows, :] = jnp.dot(n, wv[...], preferred_element_type=F32).astype(BF16)
+
+            v = vb[m, at_rows, :]
+            ll[m, at_rows, :] = jnp.where(core == 0, n, g)
+            lo[m, at_rows, :] = jnp.where(core == 0, g, n)
+            rr[m, at_rows, :] = jnp.where(core == 0, gv, v)
+            ro[m, at_rows, :] = jnp.where(core == 0, v, gv)
+            left_copy(k).start()
+            right_copy(k).start()
 
         @pl.when(k == per_micro + 1)
         def _():
-            accumulate(0, True)
+            with jax.named_scope("acc"):
+                accumulate(0, True)
 
         if micro > 2:
 
             @pl.when(jnp.logical_and(lax.rem(k, per_micro) == 1, k > 2 * per_micro))
             def _():
-                accumulate(m - 1, False)
+                with jax.named_scope("acc"):
+                    accumulate(m - 1, False)
 
     own_gain = jnp.sum(gacc[...], axis=0, keepdims=True)
     gc[core] = own_gain
@@ -253,7 +298,7 @@
     )
     gc_copy.start()
 
-    accumulate(micro - 1, False)
+    received(micro - 1)
 
     def pieces(y, z, x):
         p = (y * NZ + z) * NX + x
@@ -302,38 +347,42 @@
     def neighbours(i, n):
         return lax.rem(i + 1, n), lax.rem(i + 3, n), lax.rem(i + 2, n)
 
-    for part in range(2):
-        plus, minus, across = neighbours(*dims[part][:2])
-        stage_first(part, across, (0, 1))
-        first[part][0].start()
-        first[part][1].start()
-    for part in range(2):
-        plus, minus, across = neighbours(*dims[part][:2])
-        stage_first(part, plus, (1,))
-        first[part][2].start()
-        stage_first(part, minus, (0,))
-        first[part][3].start()
-
-    gc_copy.wait_recv()
-    gx[xi] = gc[0] + gc[1]
-    gx_copies = []
-    for d in range(1, NX):
-        copy = pltpu.make_async_remote_copy(
-            src_ref=gx.at[xi],
-            dst_ref=gx.at[xi],
-            send_sem=gx_send.at[d],
-            recv_sem=gx_recv.at[xi],
-            device_id=x_peer[d],
-            device_id_type=MESH,
-        )
-        copy.start()
-        gx_copies.append(copy)
-
-    for part in range(2):
-        plus, minus, across = neighbours(*dims[part][:2])
-        stage_first(part, plus, (0,))
-        stage_first(part, minus, (1,))
-        stage_first(part, dims[part][0], (0, 1))
+    with jax.named_scope("stage"):
+        for part in range(2):
+            plus, minus, across = neighbours(*dims[part][:2])
+            for side in range(2):
+                lane = side * (inner // 2) + part * 2 * LANES
+                add_columns(micro - 1, pl.ds(lane, wide), False)
+            stage_first(part, across, (0, 1))
+            first[part][0].start()
+            first[part][1].start()
+            stage_first(part, plus, (1,))
+            first[part][2].start()
+            stage_first(part, minus, (0,))
+            first[part][3].start()
+
+    with jax.named_scope("gain1"):
+        gc_copy.wait_recv()
+        gx[xi] = gc[0] + gc[1]
+        gx_copies = []
+        for d in range(1, NX):
+            copy = pltpu.make_async_remote_copy(
+                src_ref=gx.at[xi],
+                dst_ref=gx.at[xi],
+                send_sem=gx_send.at[d],
+                recv_sem=gx_recv.at[xi],
+                device_id=x_peer[d],
+                device_id_type=MESH,
+            )
+            copy.start()
+            gx_copies.append(copy)
+
+    with jax.named_scope("stage2"):
+        for part in range(2):
+            plus, minus, across = neighbours(*dims[part][:2])
+            stage_first(part, plus, (0,))
+            stage_first(part, minus, (1,))
+            stage_first(part, dims[part][0], (0, 1))
 
     def hop(st, r, copies, part, mine, n, loops):
         plus, minus, across = neighbours(mine, n)
@@ -348,8 +397,21 @@
 
             copies[onward].start()
 
-    for part in range(2):
-        hop(st1, r1, first[part], part, *dims[part][:2], NY * NZ)
+    with jax.named_scope("drain1"):
+        @pl.when(sec > 0)
+        def _():
+            @pl.loop(0, chunks)
+            def _(k):
+                down(k).wait_send()
+
+        @pl.loop(0, chunks)
+        def _(k):
+            left_copy(k).wait_send()
+            right_copy(k).wait_send()
+
+    with jax.named_scope("hop1"):
+        for part in range(2):
+            hop(st1, r1, first[part], part, *dims[part][:2], NY * NZ)
 
     def gathered(buf, recv, mine, n):
         for d in range(1, n):
@@ -367,51 +429,55 @@
             total = total + buf[j]
         return total
 
-    gy[yi] = gathered(gx, gx_recv, xi, NX)
-    gy_copies = []
-    for d in range(1, NY):
-        copy = pltpu.make_async_remote_copy(
-            src_ref=gy.at[yi],
-            dst_ref=gy.at[yi],
-            send_sem=gy_send.at[d],
-            recv_sem=gy_recv.at[yi],
-            device_id=y_peer[d],
+    with jax.named_scope("gain2"):
+        gy[yi] = gathered(gx, gx_recv, xi, NX)
+        gy_copies = []
+        for d in range(1, NY):
+            copy = pltpu.make_async_remote_copy(
+                src_ref=gy.at[yi],
+                dst_ref=gy.at[yi],
+                send_sem=gy_send.at[d],
+                recv_sem=gy_recv.at[yi],
+                device_id=y_peer[d],
+                device_id_type=MESH,
+            )
+            copy.start()
+            gy_copies.append(copy)
+
+    with jax.named_scope("sum1"):
+        for part in range(2):
+            mine = dims[part][0]
+            for h, slots in ((0, (3, 4)), (1, (2, 5))):
+                for slot in slots:
+                    first[part][slot].wait_recv()
+
+                @pl.loop(0, NY * NZ)
+                def _(j):
+                    total = (
+                        st1[part, mine, h, j].astype(F32)
+                        + r1[part, slots[0], j].astype(F32)
+                        + r1[part, slots[1], j].astype(F32)
+                    )
+                    st2[part, j // NZ, h, lax.rem(j, NZ)] = total.astype(BF16)
+
+            for j in range(4):
+                second[part][j].start()
+
+    with jax.named_scope("gain3"):
+        gz[zi] = gathered(gy, gy_recv, yi, NY)
+        gz_copy = pltpu.make_async_remote_copy(
+            src_ref=gz.at[zi],
+            dst_ref=gz.at[zi],
+            send_sem=gz_send,
+            recv_sem=gz_recv,
+            device_id=z_peer,
             device_id_type=MESH,
         )
-        copy.start()
-        gy_copies.append(copy)
-
-    for part in range(2):
-        mine = dims[part][0]
-        for h, slots in ((0, (3, 4)), (1, (2, 5))):
-            for slot in slots:
-                first[part][slot].wait_recv()
-
-            @pl.loop(0, NY * NZ)
-            def _(j):
-                total = (
-                    st1[part, mine, h, j].astype(F32)
-                    + r1[part, slots[0], j].astype(F32)
-                    + r1[part, slots[1], j].astype(F32)
-                )
-                st2[part, j // NZ, h, lax.rem(j, NZ)] = total.astype(BF16)
-
-        for j in range(4):
-            second[part][j].start()
-
-    gz[zi] = gathered(gy, gy_recv, yi, NY)
-    gz_copy = pltpu.make_async_remote_copy(
-        src_ref=gz.at[zi],
-        dst_ref=gz.at[zi],
-        send_sem=gz_send,
-        recv_sem=gz_recv,
-        device_id=z_peer,
-        device_id_type=MESH,
-    )
-    gz_copy.start()
-
-    for part in range(2):
-        hop(st2, r2, second[part], part, *dims[1 - part][:2], NZ)
+        gz_copy.start()
+
+    with jax.named_scope("hop2"):
+        for part in range(2):
+            hop(st2, r2, second[part], part, *dims[1 - part][:2], NZ)
 
     def z_copy(part):
         return pltpu.make_async_remote_copy(
@@ -423,65 +489,64 @@
             device_id_type=MESH,
         )
 
-    for part in range(2):
-        mine = dims[1 - part][0]
-        for h, slots in ((0, (3, 4)), (1, (2, 5))):
-            for slot in slots:
-                second[part][slot].wait_recv()
-            for z in range(NZ):
-                total = (
-                    st2[part, mine, h, z].astype(F32)
-                    + r2[part, slots[0], z].astype(F32)
-                    + r2[part, slots[1], z].astype(F32)
-                )
-                st3[part, z, h] = total.astype(BF16)
-        z_copy(part).start()
-
-    for part in range(2):
-        z_copy(part).wait_recv()
-        for h in range(2):
-            total = st3[part, zi, h].astype(F32) + r3[part, h].astype(F32)
-            lane = (part * 2 + h) * LANES
-            fin[:, lane : lane + LANES] = total[:rows]
-            fin[:, inner // 2 + lane : inner // 2 + lane + LANES] = total[rows:]
-
-    low, high = fin[0:half, :], fin[half:rows, :]
-    give[...] = jnp.where(core == 0, high, low)
-    swap = pltpu.make_async_remote_copy(
-        src_ref=give,
-        dst_ref=take,
-        send_sem=f_send,
-        recv_sem=f_recv,
-        device_id=partner,
-        device_id_type=MESH,
-    )
-    swap.start()
-    keep = jnp.where(core == 0, low, high)
-    gz_copy.wait_recv()
-    og_ref[...] = gz[0] + gz[1]
-    swap.wait_recv()
-    other = take[...]
-    ov_ref[...] = jnp.where(core == 0, keep, other)
-    oo_ref[...] = jnp.where(core == 0, other, keep)
-
-    @pl.when(sec > 0)
-    def _():
-        @pl.loop(0, chunks)
-        def _(k):
-            down(k).wait_send()
-
-    @pl.loop(0, chunks)
-    def _(k):
-        left_copy(k).wait_send()
-        right_copy(k).wait_send()
-
-    for part in range(2):
-        for j in range(6):
-            first[part][j].wait_send()
-            second[part][j].wait_send()
-        z_copy(part).wait_send()
-    for copy in [gc_copy, gz_copy, swap] + gx_copies + gy_copies:
-        copy.wait_send()
+    with jax.named_scope("sum2"):
+        for part in range(2):
+            mine = dims[1 - part][0]
+            for h, slots in ((0, (3, 4)), (1, (2, 5))):
+                for slot in slots:
+                    second[part][slot].wait_recv()
+                for z in range(NZ):
+                    total = (
+                        st2[part, mine, h, z].astype(F32)
+                        + r2[part, slots[0], z].astype(F32)
+                        + r2[part, slots[1], z].astype(F32)
+                    )
+                    st3[part, z, h] = total.astype(BF16)
+            z_copy(part).start()
+
+    with jax.named_scope("zsum"):
+        for part in range(2):
+            z_copy(part).wait_recv()
+            for h in range(2):
+                total = st3[part, zi, h].astype(F32) + r3[part, h].astype(F32)
+                lane = (part * 2 + h) * LANES
+                fin[:, lane : lane + LANES] = total[:rows]
+                fin[:, inner // 2 + lane : inner // 2 + lane + LANES] = total[rows:]
+
+    with jax.named_scope("swap"):
+        low, high = fin[0:half, :], fin[half:rows, :]
+        give[...] = jnp.where(core == 0, high, low)
+        swap = pltpu.make_async_remote_copy(
+            src_ref=give,
+            dst_ref=take,
+            send_sem=f_send,
+            recv_sem=f_recv,
+            device_id=partner,
+            device_id_type=MESH,
+        )
+        swap.start()
+        keep = jnp.where(core == 0, low, high)
+        gz_copy.wait_recv()
+        og_ref[...] = gz[0] + gz[1]
+        swap.wait_recv()
+        other = take[...]
+        ov_ref[...] = jnp.where(core == 0, keep, other)
+        oo_ref[...] = jnp.where(core == 0, other, keep)
+
+    with jax.named_scope("drain2"):
+        for part in range(2):
+            for j in range(6):
+                first[part][j].wait_send()
+                second[part][j].wait_send()
+            z_copy(part).wait_send()
+        for copy in [gc_copy, gz_copy, swap] + gx_copies + gy_copies:
+            copy.wait_send()
+
+
+def hand_out(ov, oo, og, ov_out, oo_out, og_out):
+    ov_out[:, 0, :] = ov[...]
+    oo_out[:, 0, :] = oo[...]
+    og_out[...] = og[...]
 
 
 def per_device(sections, saved, cotangent, slot_table, gain, value_weight, out_weight):
@@ -508,6 +573,9 @@
             pltpu.VMEM((micro, tokens, width), BF16),
             pltpu.VMEM((width, inner), BF16),
             pltpu.VMEM((width, inner), BF16),
+            pltpu.VMEM((inner, width), BF16),
+            pltpu.VMEM((micro, tokens, width), BF16),
+            pltpu.VMEM((micro, tokens, inner), BF16),
             pltpu.VMEM((micro, tokens, width), BF16),
             pltpu.VMEM((micro, 2 * tokens, width), BF16),
             pltpu.VMEM((micro, 2 * tokens, inner), BF16),
@@ -556,7 +624,17 @@
             collective_id=0, has_side_effects=True, vmem_limit_bytes=62 * 1024 * 1024
         ),
     )(slot_table, gain, saved[0], cotangent, value_weight[0], out_weight[0])
-    return (ov[None], oo[None], og)
+    ov, oo, og = pl.pallas_call(
+        hand_out,
+        out_shape=(
+            jax.ShapeDtypeStruct((rows // NC, 1, inner), F32),
+            jax.ShapeDtypeStruct((rows // NC, 1, inner), F32),
+            jax.ShapeDtypeStruct((1, width), F32),
+        ),
+        in_specs=[vmem, vmem, vmem],
+        out_specs=(vmem, vmem, vmem),
+    )(ov, oo, og)
+    return (jnp.transpose(ov, (1, 0, 2)), jnp.transpose(oo, (1, 0, 2)), og)
 
 
 def solution(mesh):

time: 178 us -> 164 us (0.921)
  Pallas kernels: 170 us -> 162 us
  local copies, waits for them, and re-layouts: 4.75 us -> 0 us
    pallas_call x1, Pallas kernels: 170 us -> 160 us  [per_device(): pl.pallas_call(functools.partial(kernel, sections), out_shape=(jax.ShapeD...]
    unnamed x3 -> x0, local copies, waits for them, and re-layouts: 4.75 us -> none
where the time goes in v2:
time: 164 us; the launch traced here: 162 us
  Pallas kernels  162 us (99%)
    pallas_call x1, Pallas kernels, per_device(): pl.pallas_call(functools.partial(kernel, sections), out_shape=(jax.ShapeD...  160 us

profile of v2, /device:TPU:1, one launch (start us, length us, event | category | flops | bytes accessed | tf_op | source)
XLA Modules:
  0.0 162.2 jit_solution(1364639422832456942)
XLA Ops:
  0.6 159.8 %shard_map.85 = (f32[36,1024]{1,0:T(8,128)}, f32[36,1024]{1,0:T(8,128)}, f32[1,2304]{1,0:T(1,128)}) custom-call(s32[1,3]{1,0:T(1,128)} %slot_ref.1, f32[1,2304]{1,0:T(1,128)} %gain_ref.1, bf16[3,128,2304]{2,1,0:T(8,128)(2,1)} %bitcast.7, bf16[3,128,2304]{2,1,0:T(8,128)(2,1)} %cot_hbm.1, bf16[2304,1024]{1,0:T(8,128)(2,1)} %bitcast.5, bf16[2304,1024]{1,0:T(8,128)(2,1)} %bitcast.6), custom_call_target="tpu_custom_call" | custom-call | tf_op jit(solution)/shard_map/pallas_call | solution.py:562
  160.5 1.7 %shard_map.86 = (f32[36,1,1024]{2,1,0:T(1,128)}, f32[36,1,1024]{2,1,0:T(1,128)}, f32[1,2304]{1,0:T(1,128)}) custom-call(f32[36,1024]{1,0:T(8,128)} %get-tuple-element.9.ov, f32[36,1024]{1,0:T(8,128)} %get-tuple-element.10.oo, f32[1,2304]{1,0:T(1,128)} %get-tuple-element.11.og), custom_call_target="tpu_custom_call" | custom-call | tf_op jit(solution)/shard_map/pallas_call | solution.py:627

commit v3 on v2

--- a/solution.py
+++ b/solution.py
@@ -78,6 +78,7 @@
     gy_recv,
     gz_send,
     gz_recv,
+    turn,
 ):
     micro, tokens, width = xb.shape
     inner = wv.shape[1]
@@ -256,6 +257,19 @@
                 part = part + gu_terms[8 * j : 8 * j + 8]
             gacc[...] += part
 
+        with jax.named_scope("turn"):
+
+            @pl.when(jnp.logical_and(is_top, k > 0))
+            def _():
+                @pl.when(zi == 0)
+                def _():
+                    down(k - 1).wait_send()
+                    pl.semaphore_signal(turn, inc=1, device_id=z_peer, device_id_type=MESH)
+
+                @pl.when(zi == 1)
+                def _():
+                    pl.semaphore_wait(turn, 1)
+
         @pl.when(sec > 0)
         def _():
             down(k).start()
@@ -356,11 +370,6 @@
             stage_first(part, across, (0, 1))
             first[part][0].start()
             first[part][1].start()
-            stage_first(part, plus, (1,))
-            first[part][2].start()
-            stage_first(part, minus, (0,))
-            first[part][3].start()
-
     with jax.named_scope("gain1"):
         gc_copy.wait_recv()
         gx[xi] = gc[0] + gc[1]
@@ -380,9 +389,13 @@
     with jax.named_scope("stage2"):
         for part in range(2):
             plus, minus, across = neighbours(*dims[part][:2])
-            stage_first(part, plus, (0,))
-            stage_first(part, minus, (1,))
+            stage_first(part, plus, (1, 0))
+            stage_first(part, minus, (0, 1))
             stage_first(part, dims[part][0], (0, 1))
+        for part in range(2):
+            for j in range(2):
+                first[part][j].wait_send()
+                first[part][2 + j].start()
 
     def hop(st, r, copies, part, mine, n, loops):
         plus, minus, across = neighbours(mine, n)
@@ -398,11 +411,17 @@
             copies[onward].start()
 
     with jax.named_scope("drain1"):
+        paced = jnp.logical_and(is_top, zi == 0)
+
+        @pl.when(jnp.logical_and(sec > 0, jnp.logical_not(paced)))
+        def _():
+            @pl.loop(0, chunks - 1)
+            def _(k):
+                down(k).wait_send()
+
         @pl.when(sec > 0)
         def _():
-            @pl.loop(0, chunks)
-            def _(k):
-                down(k).wait_send()
+            down(chunks - 1).wait_send()
 
         @pl.loop(0, chunks)
         def _(k):
@@ -536,7 +555,8 @@
     with jax.named_scope("drain2"):
         for part in range(2):
             for j in range(6):
-                first[part][j].wait_send()
+                if j > 1:
+                    first[part][j].wait_send()
                 second[part][j].wait_send()
             z_copy(part).wait_send()
         for copy in [gc_copy, gz_copy, swap] + gx_copies + gy_copies:
@@ -619,6 +639,7 @@
             dma((NY,)),
             dma,
             dma,
+            pltpu.SemaphoreType.REGULAR,
         ],
         compiler_params=pltpu.CompilerParams(
             collective_id=0, has_side_effects=True, vmem_limit_bytes=62 * 1024 * 1024

time: 164 us -> 156 us (0.951)
  Pallas kernels: 162 us -> 154 us
    pallas_call x1, Pallas kernels: 160 us -> 152 us  [per_device(): pl.pallas_call(functools.partial(kernel, sections), out_shape=(jax.ShapeD...]
where the time goes in v3:
time: 156 us; the launch traced here: 154 us
  Pallas kernels  154 us (99%)
    pallas_call x1, Pallas kernels, per_device(): pl.pallas_call(functools.partial(kernel, sections), out_shape=(jax.ShapeD...  152 us

profile of v3, /device:TPU:1, one launch (start us, length us, event | category | flops | bytes accessed | tf_op | source)
XLA Modules:
  0.0 154.4 jit_solution(3259098855686273910)
XLA Ops:
  0.6 152.0 %shard_map.85 = (f32[36,1024]{1,0:T(8,128)}, f32[36,1024]{1,0:T(8,128)}, f32[1,2304]{1,0:T(1,128)}) custom-call(s32[1,3]{1,0:T(1,128)} %slot_ref.1, f32[1,2304]{1,0:T(1,128)} %gain_ref.1, bf16[3,128,2304]{2,1,0:T(8,128)(2,1)} %bitcast.7, bf16[3,128,2304]{2,1,0:T(8,128)(2,1)} %cot_hbm.1, bf16[2304,1024]{1,0:T(8,128)(2,1)} %bitcast.5, bf16[2304,1024]{1,0:T(8,128)(2,1)} %bitcast.6), custom_call_target="tpu_custom_call" | custom-call | tf_op jit(solution)/shard_map/pallas_call | solution.py:582
  152.6 1.7 %shard_map.86 = (f32[36,1,1024]{2,1,0:T(1,128)}, f32[36,1,1024]{2,1,0:T(1,128)}, f32[1,2304]{1,0:T(1,128)}) custom-call(f32[36,1024]{1,0:T(8,128)} %get-tuple-element.9.ov, f32[36,1024]{1,0:T(8,128)} %get-tuple-element.10.oo, f32[1,2304]{1,0:T(1,128)} %get-tuple-element.11.og), custom_call_target="tpu_custom_call" | custom-call | tf_op jit(solution)/shard_map/pallas_call | solution.py:648

commit v4 on v3

--- a/solution.py
+++ b/solution.py
@@ -79,6 +79,9 @@
     gz_send,
     gz_recv,
     turn,
+    ub,
+    u_recv,
+    u_send,
 ):
     micro, tokens, width = xb.shape
     inner = wv.shape[1]
@@ -86,6 +89,8 @@
     chunks = micro * per_micro
     rows = width // (NY * NZ * NX)
     half = rows // NC
+    ups = chunks // 4
+    downs = chunks - ups
 
     sec = lax.axis_index("section")
     q = lax.axis_index("seq")
@@ -103,6 +108,12 @@
     z_peer = at(yi, 1 - zi, xi, core)
     above = (lax.rem(sec + 1, sections), q)
     below = (lax.rem(sec + sections - 1, sections), q)
+
+    def along_z(steps):
+        z = lax.rem(sec * NZ + zi + steps, sections * NZ)
+        return (z // NZ, ((yi * NZ + lax.rem(z, NZ)) * NX + xi) * NC + core)
+
+    up_far, down_far = along_z(3), along_z(sections * NZ - 3)
 
     wo_load = pltpu.make_async_copy(wo_hbm, wo, load_sem.at[0])
     x_load = pltpu.make_async_copy(x_hbm, xb, load_sem.at[1])
@@ -126,6 +137,45 @@
             device_id_type=MESH,
         )
 
+    def up(n):
+        m, at_rows = chunk_of(downs + n)
+        return pltpu.make_async_remote_copy(
+            src_ref=gout.at[m, at_rows],
+            dst_ref=ub.at[n],
+            send_sem=g_send.at[downs + n],
+            recv_sem=u_recv.at[n],
+            device_id=up_far,
+            device_id_type=MESH,
+        )
+
+    def onward(n):
+        m, at_rows = chunk_of(downs + n)
+        return pltpu.make_async_remote_copy(
+            src_ref=ub.at[n],
+            dst_ref=gb.at[m, at_rows],
+            send_sem=u_send.at[n],
+            recv_sem=g_recv.at[downs + n],
+            device_id=up_far,
+            device_id_type=MESH,
+        )
+
+    def relay(n):
+        with jax.named_scope("relay"):
+            up(n).wait_recv()
+            onward(n).start()
+
+    never = 4 * chunks
+    relay_odd = jnp.where(sec == 0, -ups, jnp.where(sec == 2, 8, jnp.where(sec == 3, 7, never)))
+    relay_even = jnp.where(sec == 0, 0, jnp.where(sec == 1, -1, jnp.where(sec == 3, 9, never)))
+    relay_at = jnp.where(zi == 1, relay_odd, relay_even)
+    lead = sections - sec
+
+    def order(i):
+        j = i - lead
+        mixed = jnp.where(lax.rem(j, 2) == 0, downs + j // 2, lead + (j - 1) // 2)
+        late = jnp.where(j < 2 * ups - 1, mixed, i - ups)
+        return jnp.where(i < lead, i, late)
+
     is_top = sec == sections - 1
     wv_load.start()
 
@@ -139,7 +189,7 @@
     x_load.start()
 
     barrier = pltpu.get_barrier_semaphore()
-    peers = [above, below, partner, z_peer] + x_peer[1:] + y_peer[1:]
+    peers = [above, below, up_far, down_far, partner, z_peer] + x_peer[1:] + y_peer[1:]
     for peer in peers:
         pl.semaphore_signal(barrier, inc=1, device_id=peer, device_id_type=MESH)
 
@@ -229,9 +279,17 @@
         def _(c):
             add_columns(m, pl.ds(pl.multiple_of(c * wide, wide), wide), first)
 
+    @pl.loop(0, ups)
+    def _(n):
+        @pl.when(n < -relay_at)
+        def _():
+            relay(n)
+
     @pl.loop(0, chunks)
-    def _(k):
+    def _(i):
+        k = order(i)
         m, at_rows = chunk_of(k)
+        pm, p_rows = chunk_of(i)
 
         with jax.named_scope("gwait"):
 
@@ -259,7 +317,7 @@
 
         with jax.named_scope("turn"):
 
-            @pl.when(jnp.logical_and(is_top, k > 0))
+            @pl.when(jnp.logical_and(is_top, jnp.logical_and(k > 0, k < downs)))
             def _():
                 @pl.when(zi == 0)
                 def _():
@@ -270,9 +328,13 @@
                 def _():
                     pl.semaphore_wait(turn, 1)
 
-        @pl.when(sec > 0)
+        @pl.when(jnp.logical_and(sec > 0, k < downs))
         def _():
             down(k).start()
+
+        @pl.when(jnp.logical_and(sec > 0, k >= downs))
+        def _():
+            up(k - downs).start()
 
         with jax.named_scope("share"):
 
@@ -281,24 +343,28 @@
                 vb[m, at_rows, :] = jnp.dot(n, wv[...], preferred_element_type=F32).astype(BF16)
 
             v = vb[m, at_rows, :]
-            ll[m, at_rows, :] = jnp.where(core == 0, n, g)
-            lo[m, at_rows, :] = jnp.where(core == 0, g, n)
-            rr[m, at_rows, :] = jnp.where(core == 0, gv, v)
-            ro[m, at_rows, :] = jnp.where(core == 0, v, gv)
-            left_copy(k).start()
-            right_copy(k).start()
-
-        @pl.when(k == per_micro + 1)
+            ll[pm, p_rows, :] = jnp.where(core == 0, n, g)
+            lo[pm, p_rows, :] = jnp.where(core == 0, g, n)
+            rr[pm, p_rows, :] = jnp.where(core == 0, gv, v)
+            ro[pm, p_rows, :] = jnp.where(core == 0, v, gv)
+            left_copy(i).start()
+            right_copy(i).start()
+
+        @pl.when(jnp.logical_and(i >= relay_at, i < relay_at + ups))
+        def _():
+            relay(i - relay_at)
+
+        @pl.when(i == per_micro + 1)
         def _():
             with jax.named_scope("acc"):
                 accumulate(0, True)
 
         if micro > 2:
 
-            @pl.when(jnp.logical_and(lax.rem(k, per_micro) == 1, k > 2 * per_micro))
+            @pl.when(jnp.logical_and(lax.rem(i, per_micro) == 1, i > 2 * per_micro))
             def _():
                 with jax.named_scope("acc"):
-                    accumulate(m - 1, False)
+                    accumulate(pm - 1, False)
 
     own_gain = jnp.sum(gacc[...], axis=0, keepdims=True)
     gc[core] = own_gain
@@ -415,13 +481,23 @@
 
         @pl.when(jnp.logical_and(sec > 0, jnp.logical_not(paced)))
         def _():
-            @pl.loop(0, chunks - 1)
+            @pl.loop(0, downs - 1)
             def _(k):
                 down(k).wait_send()
 
         @pl.when(sec > 0)
         def _():
-            down(chunks - 1).wait_send()
+            down(downs - 1).wait_send()
+
+            @pl.loop(0, ups)
+            def _(n):
+                up(n).wait_send()
+
+        @pl.when(relay_at < never)
+        def _():
+            @pl.loop(0, ups)
+            def _(n):
+                onward(n).wait_send()
 
         @pl.loop(0, chunks)
         def _(k):
@@ -640,6 +716,9 @@
             dma,
             dma,
             pltpu.SemaphoreType.REGULAR,
+            pltpu.VMEM((chunks // 4, CHUNK, width), BF16),
+            dma((chunks // 4,)),
+            dma((chunks // 4,)),
         ],
         compiler_params=pltpu.CompilerParams(
             collective_id=0, has_side_effects=True, vmem_limit_bytes=62 * 1024 * 1024

time: 156 us -> 146 us (0.936)
  Pallas kernels: 154 us -> 143 us
    pallas_call x1, Pallas kernels: 152 us -> 142 us  [per_device(): pl.pallas_call(functools.partial(kernel, sections), out_shape=(jax.ShapeD...]
where the time goes in v4:
time: 146 us; the launch traced here: 144 us
  Pallas kernels  143 us (98%)
    pallas_call x1, Pallas kernels, per_device(): pl.pallas_call(functools.partial(kernel, sections), out_shape=(jax.ShapeD...  142 us

profile of v4, /device:TPU:1, one launch (start us, length us, event | category | flops | bytes accessed | tf_op | source)
XLA Modules:
  0.0 144.0 jit_solution(2389008933297622547)
XLA Ops:
  0.6 141.7 %shard_map.85 = (f32[36,1024]{1,0:T(8,128)}, f32[36,1024]{1,0:T(8,128)}, f32[1,2304]{1,0:T(1,128)}) custom-call(s32[1,3]{1,0:T(1,128)} %slot_ref.1, f32[1,2304]{1,0:T(1,128)} %gain_ref.1, bf16[3,128,2304]{2,1,0:T(8,128)(2,1)} %bitcast.7, bf16[3,128,2304]{2,1,0:T(8,128)(2,1)} %cot_hbm.1, bf16[2304,1024]{1,0:T(8,128)(2,1)} %bitcast.5, bf16[2304,1024]{1,0:T(8,128)(2,1)} %bitcast.6), custom_call_target="tpu_custom_call" | custom-call | tf_op jit(solution)/shard_map/pallas_call | solution.py:658
  142.3 1.7 %shard_map.86 = (f32[36,1,1024]{2,1,0:T(1,128)}, f32[36,1,1024]{2,1,0:T(1,128)}, f32[1,2304]{1,0:T(1,128)}) custom-call(f32[36,1024]{1,0:T(8,128)} %get-tuple-element.9.ov, f32[36,1024]{1,0:T(8,128)} %get-tuple-element.10.oo, f32[1,2304]{1,0:T(1,128)} %get-tuple-element.11.og), custom_call_target="tpu_custom_call" | custom-call | tf_op jit(solution)/shard_map/pallas_call | solution.py:727

commit v5 on v4

--- a/solution.py
+++ b/solution.py
@@ -15,6 +15,8 @@
 CHUNK = 32
 NY, NZ, NX, NC = 4, 2, 4, 2
 LANES = 128
+HALF_ROWS = 112
+PAIR_ROWS = 32
 
 
 def kernel(
@@ -48,6 +50,12 @@
     r2,
     st3,
     r3,
+    stc,
+    rc,
+    st4,
+    r4,
+    st5,
+    r5,
     fin,
     give,
     take,
@@ -68,6 +76,12 @@
     s2_recv,
     s3_send,
     s3_recv,
+    sc_send,
+    sc_recv,
+    s4_send,
+    s4_recv,
+    s5_send,
+    s5_recv,
     f_send,
     f_recv,
     gc_send,
@@ -384,18 +398,32 @@
         p = (y * NZ + z) * NX + x
         return pl.ds(pl.multiple_of(p * rows, 8), rows)
 
-    def stage_first(part, dest, hs):
-        lane0 = part * 2 * LANES
-
+    def group(block_rows, g):
+        lane = g * LANES
+        top = acc[block_rows, lane : lane + LANES]
+        bottom = acc[block_rows, inner // 2 + lane : inner // 2 + lane + LANES]
+        return jnp.concatenate([top, bottom], axis=0)
+
+    def stage_ring(part, dest, hs):
         @pl.loop(0, NY * NZ)
         def _(j):
             other, z = j // NZ, lax.rem(j, NZ)
             block_rows = pieces(other, z, dest) if part == 0 else pieces(dest, z, other)
-            for h in hs:
-                lane = lane0 + h * LANES
-                top = acc[block_rows, lane : lane + LANES]
-                bottom = acc[block_rows, inner // 2 + lane : inner // 2 + lane + LANES]
-                st1[part, dest, h, j] = jnp.concatenate([top, bottom], axis=0).astype(BF16)
+            first_group = group(block_rows, 2 * part)
+            if 0 in hs:
+                st1[part, dest, 0, j] = first_group[:HALF_ROWS].astype(BF16)
+            if 1 in hs:
+                rest = group(block_rows, 2 * part + 1)[: 2 * HALF_ROWS - 2 * rows]
+                st1[part, dest, 1, j] = jnp.concatenate(
+                    [first_group[HALF_ROWS:], rest], axis=0
+                ).astype(BF16)
+
+    def stage_pair(part, dest):
+        @pl.loop(0, NY * NX)
+        def _(j):
+            block_rows = pieces(j // NX, dest, lax.rem(j, NX))
+            rest = group(block_rows, 2 * part + 1)[2 * rows - 2 * PAIR_ROWS :]
+            stc[part, dest, j] = rest.astype(BF16)
 
     def ring_copy(st, r, send, recv, part, slot, src, h, peer):
         return pltpu.make_async_remote_copy(
@@ -407,8 +435,11 @@
             device_id_type=MESH,
         )
 
+    def neighbours(i, n):
+        return lax.rem(i + 1, n), lax.rem(i + 3, n), lax.rem(i + 2, n)
+
     def ring(st, r, send, recv, part, mine, n, peer):
-        plus, minus, across = lax.rem(mine + 1, n), lax.rem(mine + 3, n), lax.rem(mine + 2, n)
+        plus, minus, across = neighbours(mine, n)
         to_plus, to_minus = peer[1], peer[3]
         copy = functools.partial(ring_copy, st, r, send, recv, part)
         return [
@@ -420,52 +451,9 @@
             copy(5, minus, 1, to_minus),
         ]
 
-    dims = [(xi, NX, x_peer), (yi, NY, y_peer)]
-    first = [ring(st1, r1, s1_send, s1_recv, part, *dims[part]) for part in range(2)]
-    second = [ring(st2, r2, s2_send, s2_recv, part, *dims[1 - part]) for part in range(2)]
-
-    def neighbours(i, n):
-        return lax.rem(i + 1, n), lax.rem(i + 3, n), lax.rem(i + 2, n)
-
-    with jax.named_scope("stage"):
-        for part in range(2):
-            plus, minus, across = neighbours(*dims[part][:2])
-            for side in range(2):
-                lane = side * (inner // 2) + part * 2 * LANES
-                add_columns(micro - 1, pl.ds(lane, wide), False)
-            stage_first(part, across, (0, 1))
-            first[part][0].start()
-            first[part][1].start()
-    with jax.named_scope("gain1"):
-        gc_copy.wait_recv()
-        gx[xi] = gc[0] + gc[1]
-        gx_copies = []
-        for d in range(1, NX):
-            copy = pltpu.make_async_remote_copy(
-                src_ref=gx.at[xi],
-                dst_ref=gx.at[xi],
-                send_sem=gx_send.at[d],
-                recv_sem=gx_recv.at[xi],
-                device_id=x_peer[d],
-                device_id_type=MESH,
-            )
-            copy.start()
-            gx_copies.append(copy)
-
-    with jax.named_scope("stage2"):
-        for part in range(2):
-            plus, minus, across = neighbours(*dims[part][:2])
-            stage_first(part, plus, (1, 0))
-            stage_first(part, minus, (0, 1))
-            stage_first(part, dims[part][0], (0, 1))
-        for part in range(2):
-            for j in range(2):
-                first[part][j].wait_send()
-                first[part][2 + j].start()
-
     def hop(st, r, copies, part, mine, n, loops):
         plus, minus, across = neighbours(mine, n)
-        for slot, dest, h, onward in ((0, plus, 0, 4), (1, minus, 1, 5)):
+        for slot, dest, h, forward in ((0, plus, 0, 4), (1, minus, 1, 5)):
             copies[slot].wait_recv()
 
             @pl.loop(0, loops)
@@ -474,35 +462,115 @@
                     st[part, dest, h, j].astype(F32) + r[part, slot, j].astype(F32)
                 ).astype(BF16)
 
-            copies[onward].start()
-
-    with jax.named_scope("drain1"):
-        paced = jnp.logical_and(is_top, zi == 0)
-
-        @pl.when(jnp.logical_and(sec > 0, jnp.logical_not(paced)))
-        def _():
-            @pl.loop(0, downs - 1)
-            def _(k):
-                down(k).wait_send()
-
-        @pl.when(sec > 0)
-        def _():
-            down(downs - 1).wait_send()
-
-            @pl.loop(0, ups)
-            def _(n):
-                up(n).wait_send()
-
-        @pl.when(relay_at < never)
-        def _():
-            @pl.loop(0, ups)
-            def _(n):
-                onward(n).wait_send()
-
-        @pl.loop(0, chunks)
+            copies[forward].start()
+
+    def collect(st, r, copies, part, mine, loops, put):
+        for h, slots in ((0, (3, 4)), (1, (2, 5))):
+            for slot in slots:
+                copies[slot].wait_recv()
+
+            @pl.loop(0, loops)
+            def _(j):
+                put(
+                    h,
+                    j,
+                    st[part, mine, h, j].astype(F32)
+                    + r[part, slots[0], j].astype(F32)
+                    + r[part, slots[1], j].astype(F32),
+                )
+
+    dims = [(xi, NX, x_peer), (yi, NY, y_peer)]
+    first = [ring(st1, r1, s1_send, s1_recv, part, *dims[part]) for part in range(2)]
+    second = [ring(st2, r2, s2_send, s2_recv, part, *dims[1 - part]) for part in range(2)]
+    fourth = [ring(st4, r4, s4_send, s4_recv, part, *dims[part]) for part in range(2)]
+    fifth = [ring(st5, r5, s5_send, s5_recv, part, *dims[1 - part]) for part in range(2)]
+
+    def pair_copy(part):
+        return pltpu.make_async_remote_copy(
+            src_ref=stc.at[part, 1 - zi],
+            dst_ref=rc.at[part],
+            send_sem=sc_send.at[part],
+            recv_sem=sc_recv.at[part],
+            device_id=z_peer,
+            device_id_type=MESH,
+        )
+
+    def z_copy(part):
+        return pltpu.make_async_remote_copy(
+            src_ref=st3.at[part, 1 - zi],
+            dst_ref=r3.at[part],
+            send_sem=s3_send.at[part],
+            recv_sem=s3_recv.at[part],
+            device_id=z_peer,
+            device_id_type=MESH,
+        )
+
+    with jax.named_scope("stage"):
+        for part in range(2):
+            plus, minus, across = neighbours(*dims[part][:2])
+            for side in range(2):
+                lane = side * (inner // 2) + part * 2 * LANES
+                add_columns(micro - 1, pl.ds(lane, wide), False)
+            stage_ring(part, across, (0, 1))
+            first[part][0].start()
+            first[part][1].start()
+            stage_pair(part, 1 - zi)
+            pair_copy(part).start()
+
+    gc_copy.wait_recv()
+    gx[xi] = gc[0] + gc[1]
+    gx_copies = []
+    for d in range(1, NX):
+        copy = pltpu.make_async_remote_copy(
+            src_ref=gx.at[xi],
+            dst_ref=gx.at[xi],
+            send_sem=gx_send.at[d],
+            recv_sem=gx_recv.at[xi],
+            device_id=x_peer[d],
+            device_id_type=MESH,
+        )
+        copy.start()
+        gx_copies.append(copy)
+
+    with jax.named_scope("stage2"):
+        for part in range(2):
+            plus, minus, across = neighbours(*dims[part][:2])
+            stage_ring(part, plus, (0, 1))
+            stage_ring(part, minus, (0, 1))
+        for part in range(2):
+            for j in range(2):
+                first[part][j].wait_send()
+                first[part][2 + j].start()
+        for part in range(2):
+            stage_ring(part, dims[part][0], (0, 1))
+            stage_pair(part, zi)
+
+    paced = jnp.logical_and(is_top, zi == 0)
+
+    @pl.when(jnp.logical_and(sec > 0, jnp.logical_not(paced)))
+    def _():
+        @pl.loop(0, downs - 1)
         def _(k):
-            left_copy(k).wait_send()
-            right_copy(k).wait_send()
+            down(k).wait_send()
+
+    @pl.when(sec > 0)
+    def _():
+        down(downs - 1).wait_send()
+
+        @pl.loop(0, ups)
+        def _(n):
+            up(n).wait_send()
+
+    @pl.when(relay_at < never)
+    def _():
+        @pl.loop(0, ups)
+        def _(n):
+            onward(n).wait_send()
+
+    @pl.loop(0, chunks)
+    def _(k):
+        left_copy(k).wait_send()
+        right_copy(k).wait_send()
 
     with jax.named_scope("hop1"):
         for part in range(2):
@@ -524,89 +592,122 @@
             total = total + buf[j]
         return total
 
-    with jax.named_scope("gain2"):
-        gy[yi] = gathered(gx, gx_recv, xi, NX)
-        gy_copies = []
-        for d in range(1, NY):
-            copy = pltpu.make_async_remote_copy(
-                src_ref=gy.at[yi],
-                dst_ref=gy.at[yi],
-                send_sem=gy_send.at[d],
-                recv_sem=gy_recv.at[yi],
-                device_id=y_peer[d],
-                device_id_type=MESH,
-            )
-            copy.start()
-            gy_copies.append(copy)
+    gy[yi] = gathered(gx, gx_recv, xi, NX)
+    gy_copies = []
+    for d in range(1, NY):
+        copy = pltpu.make_async_remote_copy(
+            src_ref=gy.at[yi],
+            dst_ref=gy.at[yi],
+            send_sem=gy_send.at[d],
+            recv_sem=gy_recv.at[yi],
+            device_id=y_peer[d],
+            device_id_type=MESH,
+        )
+        copy.start()
+        gy_copies.append(copy)
+
+    with jax.named_scope("pair"):
+        for part in range(2):
+            pair_copy(part).wait_recv()
+
+            @pl.loop(0, NY * NX)
+            def _(j):
+                total = (stc[part, zi, j].astype(F32) + rc[part, j].astype(F32)).astype(BF16)
+                y, x = j // NX, lax.rem(j, NX)
+                dest, other = (x, y) if part == 0 else (y, x)
+                st4[part, dest, 0, other] = total[: PAIR_ROWS]
+                st4[part, dest, 1, other] = total[PAIR_ROWS:]
+
+            for j in range(4):
+                fourth[part][j].start()
 
     with jax.named_scope("sum1"):
         for part in range(2):
-            mine = dims[part][0]
+
+            def put(h, j, total):
+                st2[part, j // NZ, h, lax.rem(j, NZ)] = total.astype(BF16)
+
+            collect(st1, r1, first[part], part, dims[part][0], NY * NZ, put)
+            for j in range(4):
+                second[part][j].start()
+
+    gz[zi] = gathered(gy, gy_recv, yi, NY)
+    gz_copy = pltpu.make_async_remote_copy(
+        src_ref=gz.at[zi],
+        dst_ref=gz.at[zi],
+        send_sem=gz_send,
+        recv_sem=gz_recv,
+        device_id=z_peer,
+        device_id_type=MESH,
+    )
+    gz_copy.start()
+
+    with jax.named_scope("hop4"):
+        for part in range(2):
+            hop(st4, r4, fourth[part], part, *dims[part][:2], NY)
+
+    for part in range(2):
+        for j in range(2, 6):
+            first[part][j].wait_send()
+        pair_copy(part).wait_send()
+
+    with jax.named_scope("hop2"):
+        for part in range(2):
+            hop(st2, r2, second[part], part, *dims[1 - part][:2], NZ)
+
+    with jax.named_scope("sum4"):
+        for part in range(2):
+
+            def put(h, j, total):
+                st5[part, j, h, 0] = total.astype(BF16)
+
+            collect(st4, r4, fourth[part], part, dims[part][0], NY, put)
+            for j in range(4):
+                fifth[part][j].start()
+
+    with jax.named_scope("sum2"):
+        for part in range(2):
+
+            def put(h, j, total):
+                st3[part, j, h] = total.astype(BF16)
+
+            collect(st2, r2, second[part], part, dims[1 - part][0], NZ, put)
+            z_copy(part).start()
+
+    with jax.named_scope("hop5"):
+        for part in range(2):
+            hop(st5, r5, fifth[part], part, *dims[1 - part][:2], 1)
+
+    for part in range(2):
+        for j in range(6):
+            second[part][j].wait_send()
+            fourth[part][j].wait_send()
+    for copy in [gc_copy] + gx_copies + gy_copies:
+        copy.wait_send()
+
+    def put_group(g, values):
+        lane = g * LANES
+        fin[:, lane : lane + LANES] = values[:rows]
+        fin[:, inner // 2 + lane : inner // 2 + lane + LANES] = values[rows:]
+
+    with jax.named_scope("sum5"):
+        for part in range(2):
+            mine = dims[1 - part][0]
+            tail = []
             for h, slots in ((0, (3, 4)), (1, (2, 5))):
                 for slot in slots:
-                    first[part][slot].wait_recv()
-
-                @pl.loop(0, NY * NZ)
-                def _(j):
-                    total = (
-                        st1[part, mine, h, j].astype(F32)
-                        + r1[part, slots[0], j].astype(F32)
-                        + r1[part, slots[1], j].astype(F32)
-                    )
-                    st2[part, j // NZ, h, lax.rem(j, NZ)] = total.astype(BF16)
-
-            for j in range(4):
-                second[part][j].start()
-
-    with jax.named_scope("gain3"):
-        gz[zi] = gathered(gy, gy_recv, yi, NY)
-        gz_copy = pltpu.make_async_remote_copy(
-            src_ref=gz.at[zi],
-            dst_ref=gz.at[zi],
-            send_sem=gz_send,
-            recv_sem=gz_recv,
-            device_id=z_peer,
-            device_id_type=MESH,
-        )
-        gz_copy.start()
-
-    with jax.named_scope("hop2"):
-        for part in range(2):
-            hop(st2, r2, second[part], part, *dims[1 - part][:2], NZ)
-
-    def z_copy(part):
-        return pltpu.make_async_remote_copy(
-            src_ref=st3.at[part, 1 - zi],
-            dst_ref=r3.at[part],
-            send_sem=s3_send.at[part],
-            recv_sem=s3_recv.at[part],
-            device_id=z_peer,
-            device_id_type=MESH,
-        )
-
-    with jax.named_scope("sum2"):
-        for part in range(2):
-            mine = dims[1 - part][0]
-            for h, slots in ((0, (3, 4)), (1, (2, 5))):
-                for slot in slots:
-                    second[part][slot].wait_recv()
-                for z in range(NZ):
-                    total = (
-                        st2[part, mine, h, z].astype(F32)
-                        + r2[part, slots[0], z].astype(F32)
-                        + r2[part, slots[1], z].astype(F32)
-                    )
-                    st3[part, z, h] = total.astype(BF16)
-            z_copy(part).start()
-
-    with jax.named_scope("zsum"):
-        for part in range(2):
+                    fifth[part][slot].wait_recv()
+                tail.append(
+                    st5[part, mine, h, 0].astype(F32)
+                    + r5[part, slots[0], 0].astype(F32)
+                    + r5[part, slots[1], 0].astype(F32)
+                )
             z_copy(part).wait_recv()
-            for h in range(2):
-                total = st3[part, zi, h].astype(F32) + r3[part, h].astype(F32)
-                lane = (part * 2 + h) * LANES
-                fin[:, lane : lane + LANES] = total[:rows]
-                fin[:, inner // 2 + lane : inner // 2 + lane + LANES] = total[rows:]
+            a0 = st3[part, zi, 0].astype(F32) + r3[part, 0].astype(F32)
+            a1 = st3[part, zi, 1].astype(F32) + r3[part, 1].astype(F32)
+            rest = 2 * rows - HALF_ROWS
+            put_group(2 * part, jnp.concatenate([a0, a1[:rest]], axis=0))
+            put_group(2 * part + 1, jnp.concatenate([a1[rest:]] + tail, axis=0))
 
     with jax.named_scope("swap"):
         low, high = fin[0:half, :], fin[half:rows, :]
@@ -631,11 +732,9 @@
     with jax.named_scope("drain2"):
         for part in range(2):
             for j in range(6):
-                if j > 1:
-                    first[part][j].wait_send()
-                second[part][j].wait_send()
+                fifth[part][j].wait_send()
             z_copy(part).wait_send()
-        for copy in [gc_copy, gz_copy, swap] + gx_copies + gy_copies:
+        for copy in [gz_copy, swap]:
             copy.wait_send()
 
 
@@ -650,7 +749,7 @@
     inner = value_weight.shape[2]
     rows = width // (NY * NZ * NX)
     chunks = micro * (tokens // CHUNK)
-    unit = (2 * rows, LANES)
+    long, short = (HALF_ROWS, LANES), (PAIR_ROWS, LANES)
     n1 = NY * NZ
     dma = pltpu.SemaphoreType.DMA
     hbm = pl.BlockSpec(memory_space=pl.ANY)
@@ -679,12 +778,18 @@
             pltpu.VMEM((micro, tokens, inner), BF16),
             pltpu.VMEM((width, inner), F32),
             pltpu.VMEM((8, width), F32),
-            pltpu.VMEM((2, 4, 2, n1) + unit, BF16),
-            pltpu.VMEM((2, 6, n1) + unit, BF16),
-            pltpu.VMEM((2, 4, 2, NZ) + unit, BF16),
-            pltpu.VMEM((2, 6, NZ) + unit, BF16),
-            pltpu.VMEM((2, NZ, 2) + unit, BF16),
-            pltpu.VMEM((2, 2) + unit, BF16),
+            pltpu.VMEM((2, 4, 2, n1) + long, BF16),
+            pltpu.VMEM((2, 6, n1) + long, BF16),
+            pltpu.VMEM((2, 4, 2, NZ) + long, BF16),
+            pltpu.VMEM((2, 6, NZ) + long, BF16),
+            pltpu.VMEM((2, NZ, 2) + long, BF16),
+            pltpu.VMEM((2, 2) + long, BF16),
+            pltpu.VMEM((2, NZ, NY * NX, 2 * PAIR_ROWS, LANES), BF16),
+            pltpu.VMEM((2, NY * NX, 2 * PAIR_ROWS, LANES), BF16),
+            pltpu.VMEM((2, 4, 2, 4) + short, BF16),
+            pltpu.VMEM((2, 6, 4) + short, BF16),
+            pltpu.VMEM((2, 4, 2, 1) + short, BF16),
+            pltpu.VMEM((2, 6, 1) + short, BF16),
             pltpu.VMEM((rows, inner), F32),
             pltpu.VMEM((rows // NC, inner), F32),
             pltpu.VMEM((rows // NC, inner), F32),
@@ -705,6 +810,12 @@
             dma((2, 6)),
             dma((2,)),
             dma((2,)),
+            dma((2,)),
+            dma((2,)),
+            dma((2, 6)),
+            dma((2, 6)),
+            dma((2, 6)),
+            dma((2, 6)),
             dma,
             dma,
             dma,

time: 146 us -> 144 us (0.986); the launches traced: 144 us -> 144 us
  no operation moved by 1% of the time
where the time goes in v5:
time: 144 us
  Pallas kernels  144 us (100%)
    pallas_call x1, Pallas kernels, per_device(): pl.pallas_call(functools.partial(kernel, sections), out_shape=(jax.ShapeD...  142 us

profile of v5, /device:TPU:1, one launch (start us, length us, event | category | flops | bytes accessed | tf_op | source)
XLA Modules:
  0.0 144.2 jit_solution(4098769967183035444)
XLA Ops:
  0.6 141.8 %shard_map.85 = (f32[36,1024]{1,0:T(8,128)}, f32[36,1024]{1,0:T(8,128)}, f32[1,2304]{1,0:T(1,128)}) custom-call(s32[1,3]{1,0:T(1,128)} %slot_ref.1, f32[1,2304]{1,0:T(1,128)} %gain_ref.1, bf16[3,128,2304]{2,1,0:T(8,128)(2,1)} %bitcast.7, bf16[3,128,2304]{2,1,0:T(8,128)(2,1)} %cot_hbm.1, bf16[2304,1024]{1,0:T(8,128)(2,1)} %bitcast.5, bf16[2304,1024]{1,0:T(8,128)(2,1)} %bitcast.6), custom_call_target="tpu_custom_call" | custom-call | tf_op jit(solution)/shard_map/pallas_call | solution.py:757
  142.4 1.7 %shard_map.86 = (f32[36,1,1024]{2,1,0:T(1,128)}, f32[36,1,1024]{2,1,0:T(1,128)}, f32[1,2304]{1,0:T(1,128)}) custom-call(f32[36,1024]{1,0:T(8,128)} %get-tuple-element.9.ov, f32[36,1024]{1,0:T(8,128)} %get-tuple-element.10.oo, f32[1,2304]{1,0:T(1,128)} %get-tuple-element.11.og), custom_call_target="tpu_custom_call" | custom-call | tf_op jit(solution)/shard_map/pallas_call | solution.py:838

commit v6 on v5

--- a/solution.py
+++ b/solution.py
@@ -180,7 +180,7 @@
 
     never = 4 * chunks
     relay_odd = jnp.where(sec == 0, -ups, jnp.where(sec == 2, 8, jnp.where(sec == 3, 7, never)))
-    relay_even = jnp.where(sec == 0, 0, jnp.where(sec == 1, -1, jnp.where(sec == 3, 9, never)))
+    relay_even = jnp.where(sec == 0, 0, jnp.where(sec == 1, -2, jnp.where(sec == 3, 9, never)))
     relay_at = jnp.where(zi == 1, relay_odd, relay_even)
     lead = sections - sec
 

time: 144 us -> 143 us (level)
  Pallas kernels: 144 us -> 142 us
where the time goes in v6:
time: 143 us
  Pallas kernels  142 us (99%)
    pallas_call x1, Pallas kernels, per_device(): pl.pallas_call(functools.partial(kernel, sections), out_shape=(jax.ShapeD...  140 us

profile of v6, /device:TPU:1, one launch (start us, length us, event | category | flops | bytes accessed | tf_op | source)
XLA Modules:
  0.0 142.8 jit_solution(10743643250430042056)
XLA Ops:
  0.6 140.4 %shard_map.85 = (f32[36,1024]{1,0:T(8,128)}, f32[36,1024]{1,0:T(8,128)}, f32[1,2304]{1,0:T(1,128)}) custom-call(s32[1,3]{1,0:T(1,128)} %slot_ref.1, f32[1,2304]{1,0:T(1,128)} %gain_ref.1, bf16[3,128,2304]{2,1,0:T(8,128)(2,1)} %bitcast.7, bf16[3,128,2304]{2,1,0:T(8,128)(2,1)} %cot_hbm.1, bf16[2304,1024]{1,0:T(8,128)(2,1)} %bitcast.5, bf16[2304,1024]{1,0:T(8,128)(2,1)} %bitcast.6), custom_call_target="tpu_custom_call" | custom-call | tf_op jit(solution)/shard_map/pallas_call | solution.py:757
  141.1 1.7 %shard_map.86 = (f32[36,1,1024]{2,1,0:T(1,128)}, f32[36,1,1024]{2,1,0:T(1,128)}, f32[1,2304]{1,0:T(1,128)}) custom-call(f32[36,1024]{1,0:T(8,128)} %get-tuple-element.9.ov, f32[36,1024]{1,0:T(8,128)} %get-tuple-element.10.oo, f32[1,2304]{1,0:T(1,128)} %get-tuple-element.11.og), custom_call_target="tpu_custom_call" | custom-call | tf_op jit(solution)/shard_map/pallas_call | solution.py:838
